TPU v7x, 32 devices: a 4x4x1 block of a 4x4x8 slice. The times are simulated.
32 devices in a mesh: rep: 1 (over z), col: 4 (over y), row: 8 (over x, core).
Axes of the slice: x: 4, y: 4, z: 1, core: 2. Of those that a mesh axis runs over, the one named last changes fastest.
The devices are a block of a 4x4x8 slice.
Arguments:
- hidden_0: bfloat16 [128, 3072], P('rep', 'row')
- hidden_1: bfloat16 [128, 3072], P('rep', 'row')
- positions: int32 [128], P(('rep', 'row'))
- lengths: int32 [128], P(('rep', 'row'))
- cache_k: bfloat16 [2, 128, 512, 8, 128], P(None, ('rep', 'row'), None, 'col')
- cache_v: bfloat16 [2, 128, 512, 8, 128], P(None, ('rep', 'row'), None, 'col')
- norm_attn: bfloat16 [2, 3072], P(None, 'row')
- norm_mlp: bfloat16 [2, 3072], P(None, 'row')
- w_query: bfloat16 [2, 3072, 3072], P(None, 'row', 'col')
- w_key: bfloat16 [2, 3072, 1024], P(None, 'row', 'col')
- w_value: bfloat16 [2, 3072, 1024], P(None, 'row', 'col')
- w_out: bfloat16 [2, 3072, 3072], P(None, 'row', 'col')
- w_gate: bfloat16 [2, 3072, 8192], P(None, 'row', 'col')
- w_up: bfloat16 [2, 3072, 8192], P(None, 'row', 'col')
- w_down: bfloat16 [2, 8192, 3072], P(None, 'row', 'col')
Outputs:
- output 1: bfloat16 [128, 3072], P('rep', 'row')
- output 2: bfloat16 [128, 3072], P('rep', 'row')
- output 3: bfloat16 [2, 128, 512, 8, 128], P(None, ('rep', 'row'), None, 'col')
- output 4: bfloat16 [2, 128, 512, 8, 128], P(None, ('rep', 'row'), None, 'col')
All inputs are finite; a program needn't handle non-finite values.
Results may differ from a plain program's by a relative error of at most 0.02.
Values are sent between devices in bfloat16 or wider.
A program may use at most 768 MiB of HBM per device.

v0:
```python
import jax
import jax.numpy as jnp
from jax import lax
from jax.sharding import PartitionSpec as P

ROPE_BASE = 1000000.0
EPS = 1e-05


def rope_rotate(vectors, positions):
    head_dim = vectors.shape[-1]
    half = head_dim // 2
    inv_freq = jnp.power(jnp.float32(ROPE_BASE), -jnp.arange(half, dtype=jnp.float32) * 2.0 / head_dim)
    angles = positions.astype(jnp.float32)[:, None, None] * inv_freq
    cosine = jnp.cos(angles)
    sine = jnp.sin(angles)
    vec_f32 = vectors.astype(jnp.float32)
    first = vec_f32[..., :half]
    second = vec_f32[..., half:]
    return jnp.concatenate([first * cosine - second * sine, second * cosine + first * sine], axis=-1).astype(jnp.bfloat16)


def add_residual(hidden, update):
    return (hidden.astype(jnp.float32) + update.astype(jnp.float32)).astype(jnp.bfloat16)


def attend_local(query, keys, vals, slots):
    scores = jnp.einsum('bkgd,blkd->bkgl', query, keys, preferred_element_type=jnp.float32) * (keys.shape[-1] ** -0.5)
    valid = jnp.arange(keys.shape[1])[None, None, None, :] <= slots[:, None, None, None]
    probs = jax.nn.softmax(jnp.where(valid, scores, -jnp.inf), axis=-1).astype(jnp.bfloat16)
    return jnp.einsum('bkgl,blkd->bkgd', probs, vals, preferred_element_type=jnp.float32).astype(jnp.bfloat16)


def solution(mesh):
    row_count = mesh.shape['row']
    hidden_spec = P('rep', 'row')
    index_spec = P(('rep', 'row'))
    cache_spec = P(None, ('rep', 'row'), None, 'col', None)
    gain_spec = P(None, 'row')
    weight_spec = P(None, 'row', 'col')

    def rms_norm(hidden, gain):
        hidden_f = hidden.astype(jnp.float32)
        square_sum = lax.psum(jnp.sum(hidden_f * hidden_f, axis=-1, keepdims=True), 'row')
        scale = lax.rsqrt(square_sum / (hidden.shape[-1] * row_count) + EPS)
        return (hidden_f * scale * gain.astype(jnp.float32)).astype(jnp.bfloat16)

    def sum_rows(partial):
        return lax.psum_scatter(partial.astype(jnp.bfloat16), 'row', scatter_dimension=0, tiled=True)

    def to_row_features(block):
        whole = lax.all_gather(block, 'col', axis=1, tiled=True)
        return lax.all_to_all(whole, 'row', 1, 0, tiled=True)

    def decoder_layer(hidden, layer, cache_k, cache_v, positions, slots, weights):
        norm_attn, norm_mlp, w_query, w_key, w_value, w_out, w_gate, w_up, w_down = weights
        head_dim = cache_k.shape[-1]
        kv_local = cache_k.shape[-2]
        q_local = w_query.shape[-1]
        kv_cols = w_key.shape[-1]
        ff_local = w_gate.shape[-1]
        normed = rms_norm(hidden, norm_attn[layer])
        qkv_part = jnp.concatenate([
            jnp.dot(normed, w_query[layer], preferred_element_type=jnp.float32),
            jnp.dot(normed, w_key[layer], preferred_element_type=jnp.float32),
            jnp.dot(normed, w_value[layer], preferred_element_type=jnp.float32)], axis=1)
        qkv_local = sum_rows(qkv_part)
        batch_local = qkv_local.shape[0]
        query = rope_rotate(qkv_local[:, :q_local].reshape(batch_local, -1, head_dim), positions)
        key_new = rope_rotate(qkv_local[:, q_local:q_local + kv_cols].reshape(batch_local, kv_local, head_dim), positions)
        value_new = qkv_local[:, q_local + kv_cols:].reshape(batch_local, kv_local, head_dim)
        rows = jnp.arange(batch_local)
        cache_k = cache_k.at[layer, rows, slots].set(key_new)
        cache_v = cache_v.at[layer, rows, slots].set(value_new)
        attended = attend_local(query.reshape(batch_local, kv_local, -1, head_dim), cache_k[layer], cache_v[layer], slots)
        attn_rows = to_row_features(attended.reshape(batch_local, -1))
        attn_out = to_row_features(sum_rows(jnp.dot(attn_rows, w_out[layer], preferred_element_type=jnp.float32)))
        hidden = add_residual(hidden, attn_out)
        normed = rms_norm(hidden, norm_mlp[layer])
        gate_up = sum_rows(jnp.concatenate([
            jnp.dot(normed, w_gate[layer], preferred_element_type=jnp.float32),
            jnp.dot(normed, w_up[layer], preferred_element_type=jnp.float32)], axis=1))
        activated = (jax.nn.silu(gate_up[:, :ff_local].astype(jnp.float32)) * gate_up[:, ff_local:].astype(jnp.float32)).astype(jnp.bfloat16)
        down_out = to_row_features(sum_rows(jnp.dot(to_row_features(activated), w_down[layer], preferred_element_type=jnp.float32)))
        return add_residual(hidden, down_out), cache_k, cache_v

    def device_program(hidden_0, hidden_1, positions, lengths, cache_k, cache_v, norm_attn, norm_mlp, w_query, w_key, w_value, w_out, w_gate, w_up, w_down):
        weights = (norm_attn, norm_mlp, w_query, w_key, w_value, w_out, w_gate, w_up, w_down)
        outputs = []
        for step, hidden in enumerate((hidden_0, hidden_1)):
            for layer in range(w_query.shape[0]):
                hidden, cache_k, cache_v = decoder_layer(hidden, layer, cache_k, cache_v, positions + step, lengths + step, weights)
            outputs.append(hidden)
        return outputs[0], outputs[1], cache_k, cache_v

    return jax.shard_map(device_program, mesh=mesh,
                         in_specs=(hidden_spec, hidden_spec, index_spec, index_spec, cache_spec, cache_spec, gain_spec, gain_spec) + (weight_spec,) * 7,
                         out_specs=(hidden_spec, hidden_spec, cache_spec, cache_spec), check_vma=False)
```

profile of v0, /device:TPU:97, one launch (start us, length us, event | category | flops | bytes accessed | tf_op | source)
XLA Modules:
  0.0 955.1 jit_solution(1670303741536928879)
XLA Ops:
  19.8 13.9 %psum.56 = f32[128,1]{0,1:T(1,128)S(1)} all-reduce(f32[128,1]{0,1:T(1,128)S(1)} %bitcast.397), channel_id=1, replica_groups=mesh['rep'=1,'col'=4,'row'=8] {'row'}, use_global_device_ids=true, to_apply=%region_1.0 | all-reduce | flops 128 | bytes 1024 | tf_op jit(solution)/shard_map/psum | solution.py:44
  35.6 27.9 %reduce-scatter.17.cloned.1.call-done = bf16[16,1280]{1,0:T(8,128)(2,1)} async-done(((bf16[128,1280]{1,0:T(8,128)(2,1)}), bf16[16,1280]{1,0:T(8,128)(2,1)}) %reduce-scatter.17.cloned.1.call-update) | async-done | bytes 40976 | tf_op jit(solution)/shard_map/reduce_scatter | solution.py:49
  101.9 13.4 %all_to_all.256 = bf16[16,8,384]{2,0,1:T(8,128)(2,1)S(1)} all-to-all(bf16[16,8,384]{2,0,1:T(8,128)(2,1)S(1)} %bitcast.359), channel_id=1, replica_groups=mesh['rep'=1,'col'=4,'row'=8] {'row'}, dimensions={1} | all-to-all | bytes 196608 | tf_op jit(solution)/shard_map/all_to_all | solution.py:53
  116.3 24.6 %reduce-scatter.19.cloned.1.call-done = bf16[16,768]{1,0:T(8,128)(2,1)} async-done(((bf16[128,768]{1,0:T(8,128)(2,1)}), bf16[16,768]{1,0:T(8,128)(2,1)}) %reduce-scatter.19.cloned.1.call-update) | async-done | bytes 24592 | tf_op jit(solution)/shard_map/reduce_scatter | solution.py:49
  165.5 12.6 %psum.57 = f32[128,1]{0,1:T(1,128)S(1)} all-reduce(f32[128,1]{0,1:T(1,128)S(1)} %bitcast.394), channel_id=1, replica_groups=mesh['rep'=1,'col'=4,'row'=8] {'row'}, use_global_device_ids=true, to_apply=%region_9.10 | all-reduce | flops 128 | bytes 1024 | tf_op jit(solution)/shard_map/psum | solution.py:44
  183.2 25.5 %reduce-scatter.21.cloned.1.call-done = bf16[16,4096]{1,0:T(8,128)(2,1)} async-done(((bf16[128,4096]{1,0:T(8,128)(2,1)}), bf16[16,4096]{1,0:T(8,128)(2,1)}) %reduce-scatter.21.cloned.1.call-update) | async-done | bytes 131088 | tf_op jit(solution)/shard_map/reduce_scatter | solution.py:49
  219.7 15.1 %all_to_all.257 = bf16[16,8,1024]{2,0,1:T(8,128)(2,1)S(1)} all-to-all(bf16[16,8,1024]{2,0,1:T(8,128)(2,1)S(1)} %bitcast.356), channel_id=1, replica_groups=mesh['rep'=1,'col'=4,'row'=8] {'row'}, dimensions={1} | all-to-all | bytes 524288 | tf_op jit(solution)/shard_map/all_to_all | solution.py:53
  237.3 24.8 %reduce-scatter.23.cloned.1.call-done = bf16[16,768]{1,0:T(8,128)(2,1)} async-done(((bf16[128,768]{1,0:T(8,128)(2,1)}), bf16[16,768]{1,0:T(8,128)(2,1)}) %reduce-scatter.23.cloned.1.call-update) | async-done | bytes 24592 | tf_op jit(solution)/shard_map/reduce_scatter | solution.py:49
  286.7 12.6 %all-reduce.1 = (f32[128,1]{0,1:T(1,128)S(1)}, f32[128,1]{0,1:T(1,128)S(1)}) all-reduce(f32[128,1]{0,1:T(1,128)S(1)} %bitcast.395, f32[128,1]{0,1:T(1,128)S(1)} %bitcast.392), channel_id=1, replica_groups=mesh['rep'=1,'col'=4,'row'=8] {'row'}, use_global_device_ids=true, to_apply=%region_13.14 | all-reduce | flops 256 | bytes 2048 | tf_op jit(solution)/shard_map/psum | solution.py:44
  304.6 21.7 %reduce-scatter.33.cloned.1.call-done = bf16[16,1280]{1,0:T(8,128)(2,1)} async-done(((bf16[128,1280]{1,0:T(8,128)(2,1)}), bf16[16,1280]{1,0:T(8,128)(2,1)}) %reduce-scatter.33.cloned.1.call-update) | async-done | bytes 40976 | tf_op jit(solution)/shard_map/reduce_scatter | solution.py:49
  327.0 28.7 %reduce-scatter.25.cloned.1.call-done = bf16[16,1280]{1,0:T(8,128)(2,1)} async-done(((bf16[128,1280]{1,0:T(8,128)(2,1)}), bf16[16,1280]{1,0:T(8,128)(2,1)}) %reduce-scatter.25.cloned.1.call-update) | async-done | bytes 40976 | tf_op jit(solution)/shard_map/reduce_scatter | solution.py:49
  413.6 13.4 %all_to_all.258 = bf16[16,8,384]{2,0,1:T(8,128)(2,1)S(1)} all-to-all(bf16[16,8,384]{2,0,1:T(8,128)(2,1)S(1)} %bitcast.361), channel_id=1, replica_groups=mesh['rep'=1,'col'=4,'row'=8] {'row'}, dimensions={1} | all-to-all | bytes 196608 | tf_op jit(solution)/shard_map/all_to_all | solution.py:53
  428.1 24.5 %reduce-scatter.35.cloned.1.call-done = bf16[16,768]{1,0:T(8,128)(2,1)} async-done(((bf16[128,768]{1,0:T(8,128)(2,1)}), bf16[16,768]{1,0:T(8,128)(2,1)}) %reduce-scatter.35.cloned.1.call-update) | async-done | bytes 24592 | tf_op jit(solution)/shard_map/reduce_scatter | solution.py:49
  462.3 13.4 %all_to_all.259 = bf16[16,8,384]{2,0,1:T(8,128)(2,1)S(1)} all-to-all(bf16[16,8,384]{2,0,1:T(8,128)(2,1)S(1)} %bitcast.363), channel_id=1, replica_groups=mesh['rep'=1,'col'=4,'row'=8] {'row'}, dimensions={1} | all-to-all | bytes 196608 | tf_op jit(solution)/shard_map/all_to_all | solution.py:53
  475.9 12.6 %psum.61 = f32[128,1]{0,1:T(1,128)S(1)} all-reduce(f32[128,1]{0,1:T(1,128)S(1)} %bitcast.396), channel_id=1, replica_groups=mesh['rep'=1,'col'=4,'row'=8] {'row'}, use_global_device_ids=true, to_apply=%region_33.34 | all-reduce | flops 128 | bytes 1024 | tf_op jit(solution)/shard_map/psum | solution.py:44
  493.6 25.5 %reduce-scatter.37.cloned.1.call-done = bf16[16,4096]{1,0:T(8,128)(2,1)} async-done(((bf16[128,4096]{1,0:T(8,128)(2,1)}), bf16[16,4096]{1,0:T(8,128)(2,1)}) %reduce-scatter.37.cloned.1.call-update) | async-done | bytes 131088 | tf_op jit(solution)/shard_map/reduce_scatter | solution.py:49
  530.3 15.1 %all_to_all.260 = bf16[16,8,1024]{2,0,1:T(8,128)(2,1)S(1)} all-to-all(bf16[16,8,1024]{2,0,1:T(8,128)(2,1)S(1)} %bitcast.357), channel_id=1, replica_groups=mesh['rep'=1,'col'=4,'row'=8] {'row'}, dimensions={1} | all-to-all | bytes 524288 | tf_op jit(solution)/shard_map/all_to_all | solution.py:53
  548.1 24.8 %reduce-scatter.39.cloned.1.call-done = bf16[16,768]{1,0:T(8,128)(2,1)} async-done(((bf16[128,768]{1,0:T(8,128)(2,1)}), bf16[16,768]{1,0:T(8,128)(2,1)}) %reduce-scatter.39.cloned.1.call-update) | async-done | bytes 24592 | tf_op jit(solution)/shard_map/reduce_scatter | solution.py:49
  582.6 13.4 %all_to_all.261 = bf16[16,8,384]{2,0,1:T(8,128)(2,1)S(1)} all-to-all(bf16[16,8,384]{2,0,1:T(8,128)(2,1)S(1)} %bitcast.364), channel_id=1, replica_groups=mesh['rep'=1,'col'=4,'row'=8] {'row'}, dimensions={1} | all-to-all | bytes 196608 | tf_op jit(solution)/shard_map/all_to_all | solution.py:53
  596.1 12.6 %psum.62 = f32[128,1]{0,1:T(1,128)S(1)} all-reduce(f32[128,1]{0,1:T(1,128)S(1)} %bitcast.398), channel_id=1, replica_groups=mesh['rep'=1,'col'=4,'row'=8] {'row'}, use_global_device_ids=true, to_apply=%region_37.38 | all-reduce | flops 128 | bytes 1024 | tf_op jit(solution)/shard_map/psum | solution.py:44
  611.4 24.3 %reduce-scatter.41.cloned.1.call-done = bf16[16,1280]{1,0:T(8,128)(2,1)} async-done(((bf16[128,1280]{1,0:T(8,128)(2,1)}), bf16[16,1280]{1,0:T(8,128)(2,1)}) %reduce-scatter.41.cloned.1.call-update) | async-done | bytes 40976 | tf_op jit(solution)/shard_map/reduce_scatter | solution.py:49
  768.5 12.6 %all-reduce = (f32[128,1]{0,1:T(1,128)S(1)}, f32[128,1]{0,1:T(1,128)S(1)}) all-reduce(f32[128,1]{0,1:T(1,128)S(1)} %bitcast.393, f32[128,1]{0,1:T(1,128)S(1)} %bitcast.391), channel_id=1, replica_groups=mesh['rep'=1,'col'=4,'row'=8] {'row'}, use_global_device_ids=true, to_apply=%region_21.22 | all-reduce | flops 256 | bytes 2048 | tf_op jit(solution)/shard_map/psum | solution.py:44
  791.2 20.6 %reduce-scatter.45.cloned.1.call-done = bf16[16,4096]{1,0:T(8,128)(2,1)} async-done(((bf16[128,4096]{1,0:T(8,128)(2,1)}), bf16[16,4096]{1,0:T(8,128)(2,1)}) %reduce-scatter.45.cloned.1.call-update) | async-done | bytes 131088 | tf_op jit(solution)/shard_map/reduce_scatter | solution.py:49
  874.1 19.7 %reduce-scatter.47.cloned.1.call-done = bf16[16,768]{1,0:T(8,128)(2,1)} async-done(((bf16[128,768]{1,0:T(8,128)(2,1)}), bf16[16,768]{1,0:T(8,128)(2,1)}) %reduce-scatter.47.cloned.1.call-update) | async-done | bytes 24592 | tf_op jit(solution)/shard_map/reduce_scatter | solution.py:49
  (263 shorter events, 486.8 us)
Async XLA Ops:
  7.2 56.4 %reduce-scatter.17.cloned.1.call-start = ((), (), s32[]{:S(2)}) async-start(), calls=%async_computation.32 | async-start | bytes 368640 | tf_op jit(solution)/shard_map/reduce_scatter | solution.py:49
  35.3 105.6 %reduce-scatter.19.cloned.1.call-start = ((), (), s32[]{:S(2)}) async-start(), calls=%async_computation.33 | async-start | bytes 221184 | tf_op jit(solution)/shard_map/reduce_scatter | solution.py:49
  151.3 14.1 %all-to-all-start.1 = ((bf16[16,8,384]{2,0,1:T(8,128)(2,1)}), bf16[16,8,384]{2,0,1:T(8,128)(2,1)S(1)}, u32[]{:S(2)}, u32[]{:S(2)}) async-start(bf16[16,8,384]{2,0,1:T(8,128)(2,1)} %bitcast.350), calls=%async_computation.3 | async-start | bytes 196608 | tf_op jit(solution)/shard_map/all_to_all | solution.py:53
  160.5 48.1 %reduce-scatter.21.cloned.1.call-start = ((), (), s32[]{:S(2)}) async-start(), calls=%async_computation.34 | async-start | bytes 1179648 | tf_op jit(solution)/shard_map/reduce_scatter | solution.py:49
  183.1 79.0 %reduce-scatter.23.cloned.1.call-start = ((), (), s32[]{:S(2)}) async-start(), calls=%async_computation.35 | async-start | bytes 221184 | tf_op jit(solution)/shard_map/reduce_scatter | solution.py:49
  281.7 44.5 %reduce-scatter.33.cloned.1.call-start = ((), (), s32[]{:S(2)}) async-start(), calls=%async_computation.40 | async-start | bytes 368640 | tf_op jit(solution)/shard_map/reduce_scatter | solution.py:49
  301.9 53.8 %reduce-scatter.25.cloned.1.call-start = ((), (), s32[]{:S(2)}) async-start(), calls=%async_computation.36 | async-start | bytes 368640 | tf_op jit(solution)/shard_map/reduce_scatter | solution.py:49
  304.4 148.2 %reduce-scatter.35.cloned.1.call-start = ((), (), s32[]{:S(2)}) async-start(), calls=%async_computation.41 | async-start | bytes 221184 | tf_op jit(solution)/shard_map/reduce_scatter | solution.py:49
  428.0 91.1 %reduce-scatter.37.cloned.1.call-start = ((), (), s32[]{:S(2)}) async-start(), calls=%async_computation.42 | async-start | bytes 1179648 | tf_op jit(solution)/shard_map/reduce_scatter | solution.py:49
  493.5 79.4 %reduce-scatter.39.cloned.1.call-start = ((), (), s32[]{:S(2)}) async-start(), calls=%async_computation.43 | async-start | bytes 221184 | tf_op jit(solution)/shard_map/reduce_scatter | solution.py:49
  548.0 87.7 %reduce-scatter.41.cloned.1.call-start = ((), (), s32[]{:S(2)}) async-start(), calls=%async_computation.44 | async-start | bytes 368640 | tf_op jit(solution)/shard_map/reduce_scatter | solution.py:49
  673.5 14.1 %all-to-all-start.12 = ((bf16[16,8,384]{2,0,1:T(8,128)(2,1)}), bf16[16,8,384]{2,0,1:T(8,128)(2,1)S(1)}, u32[]{:S(2)}, u32[]{:S(2)}) async-start(bf16[16,8,384]{2,0,1:T(8,128)(2,1)} %bitcast.342), calls=%async_computation.25 | async-start | bytes 196608 | tf_op jit(solution)/shard_map/all_to_all | solution.py:53
  682.8 31.4 %reduce-scatter.43.cloned.1.call-start = ((), (), s32[]{:S(2)}) async-start(), calls=%async_computation.45 | async-start | bytes 221184 | tf_op jit(solution)/shard_map/reduce_scatter | solution.py:49
  688.6 55.3 %reduce-scatter.27.cloned.1.call-start = ((), (), s32[]{:S(2)}) async-start(), calls=%async_computation.37 | async-start | bytes 221184 | tf_op jit(solution)/shard_map/reduce_scatter | solution.py:49
  724.8 29.2 %all-to-all-start.13 = ((bf16[16,8,384]{2,0,1:T(8,128)(2,1)}), bf16[16,8,384]{2,0,1:T(8,128)(2,1)S(1)}, u32[]{:S(2)}, u32[]{:S(2)}) async-start(bf16[16,8,384]{2,0,1:T(8,128)(2,1)} %bitcast.341), calls=%async_computation.27 | async-start | bytes 196608 | tf_op jit(solution)/shard_map/all_to_all | solution.py:53
  754.1 14.3 %all-to-all-start.5 = ((bf16[16,8,384]{2,0,1:T(8,128)(2,1)}), bf16[16,8,384]{2,0,1:T(8,128)(2,1)S(1)}, u32[]{:S(2)}, u32[]{:S(2)}) async-start(bf16[16,8,384]{2,0,1:T(8,128)(2,1)} %bitcast.347), calls=%async_computation.11 | async-start | bytes 196608 | tf_op jit(solution)/shard_map/all_to_all | solution.py:53
  763.5 48.2 %reduce-scatter.45.cloned.1.call-start = ((), (), s32[]{:S(2)}) async-start(), calls=%async_computation.46 | async-start | bytes 1179648 | tf_op jit(solution)/shard_map/reduce_scatter | solution.py:49
  786.1 58.0 %reduce-scatter.29.cloned.1.call-start = ((), (), s32[]{:S(2)}) async-start(), calls=%async_computation.38 | async-start | bytes 1179648 | tf_op jit(solution)/shard_map/reduce_scatter | solution.py:49
  823.4 32.0 %all-to-all-start.14 = ((bf16[16,8,1024]{2,0,1:T(8,128)(2,1)}), bf16[16,8,1024]{2,0,1:T(8,128)(2,1)S(1)}, u32[]{:S(2)}, u32[]{:S(2)}) async-start(bf16[16,8,1024]{2,0,1:T(8,128)(2,1)} %bitcast.336), calls=%async_computation.29 | async-start | bytes 524288 | tf_op jit(solution)/shard_map/all_to_all | solution.py:53
  855.5 16.1 %all-to-all-start.6 = ((bf16[16,8,1024]{2,0,1:T(8,128)(2,1)}), bf16[16,8,1024]{2,0,1:T(8,128)(2,1)S(1)}, u32[]{:S(2)}, u32[]{:S(2)}) async-start(bf16[16,8,1024]{2,0,1:T(8,128)(2,1)} %bitcast.338), calls=%async_computation.13 | async-start | bytes 524288 | tf_op jit(solution)/shard_map/all_to_all | solution.py:53
  865.2 28.6 %reduce-scatter.47.cloned.1.call-start = ((), (), s32[]{:S(2)}) async-start(), calls=%async_computation.47 | async-start | bytes 221184 | tf_op jit(solution)/shard_map/reduce_scatter | solution.py:49
  867.7 55.9 %reduce-scatter.31.cloned.1.call-start = ((), (), s32[]{:S(2)}) async-start(), calls=%async_computation.39 | async-start | bytes 221184 | tf_op jit(solution)/shard_map/reduce_scatter | solution.py:49
  904.2 29.2 %all-to-all-start.15 = ((bf16[16,8,384]{2,0,1:T(8,128)(2,1)}), bf16[16,8,384]{2,0,1:T(8,128)(2,1)S(1)}, u32[]{:S(2)}, u32[]{:S(2)}) async-start(bf16[16,8,384]{2,0,1:T(8,128)(2,1)} %bitcast.340), calls=%async_computation.31 | async-start | bytes 196608 | tf_op jit(solution)/shard_map/all_to_all | solution.py:53
  933.4 14.3 %all-to-all-start.7 = ((bf16[16,8,384]{2,0,1:T(8,128)(2,1)}), bf16[16,8,384]{2,0,1:T(8,128)(2,1)S(1)}, u32[]{:S(2)}, u32[]{:S(2)}) async-start(bf16[16,8,384]{2,0,1:T(8,128)(2,1)} %bitcast.346), calls=%async_computation.15 | async-start | bytes 196608 | tf_op jit(solution)/shard_map/all_to_all | solution.py:53
  (16 other events, 407.3 us)
Sparse Core Ops, SparseCore 0:
  35.4 28.1 reduce-scatter.16
  116.4 24.4 reduce-scatter.18
  183.2 25.3 reduce-scatter.20
  237.4 24.6 reduce-scatter.22
  302.0 24.2 reduce-scatter.32
  328.4 27.2 reduce-scatter.24
  428.1 24.4 reduce-scatter.34
  493.7 25.3 reduce-scatter.36
  548.1 24.7 reduce-scatter.38
  611.4 24.2 reduce-scatter.40
  688.8 25.3 reduce-scatter.42
  716.3 27.6 reduce-scatter.26
  786.2 25.4 reduce-scatter.44
  813.8 30.2 reduce-scatter.28
  867.9 25.8 reduce-scatter.46
  895.9 27.5 reduce-scatter.30
where the time goes:
time: 966 us; the launch traced here: 955 us
  waiting for transfers between devices  348 us (36%)
  blocking collectives  329 us (34%)
  local copies, waits for them, and re-layouts  97.9 us (10%)
  starting transfers between devices  85.3 us (9%)
  matrix products  61.8 us (6%)
  other arithmetic  17.9 us (2%)
  between operations  14.8 us (2%)
    reduce_scatter x16, waiting for transfers between devices, sum_rows(): lax.psum_scatter(partial.astype(jnp.bfloat16), 'row', scatter_dimension=0...  325 us
    all_gather x16, blocking collectives, to_row_features(): whole = lax.all_gather(block, 'col', axis=1, tiled=True)  156 us
    all_to_all x7, blocking collectives, to_row_features(): return lax.all_to_all(whole, 'row', 1, 0, tiled=True)  95.5 us
    all_to_all x9, starting transfers between devices, to_row_features(): return lax.all_to_all(whole, 'row', 1, 0, tiled=True)  84.1 us
    psum x6, blocking collectives, rms_norm(): lax.psum(jnp.sum(hidden_f * hidden_f, axis=-1, keepdims=True), 'row')  77.1 us
    slice x4, local copies, waits for them, and re-layouts, decoder_layer(): cache_k[layer]  28.9 us
    slice x4, local copies, waits for them, and re-layouts, decoder_layer(): cache_v[layer]  28.8 us
    all_to_all x9, waiting for transfers between devices, to_row_features(): return lax.all_to_all(whole, 'row', 1, 0, tiled=True)  22.9 us
  transfers between devices with their start and end apart: 25, of which 22 were waited for; matrix products, arithmetic and copies ran while one was open for 3% of the time, Pallas kernels for 0%

commit v1 on v0

v1 whole, which is shorter than its diff:
```python
import functools

import jax
import jax.numpy as jnp
from jax import lax
from jax.experimental import pallas as pl
from jax.experimental.pallas import tpu as pltpu
from jax.sharding import PartitionSpec as P

ROPE_BASE = 1000000.0
EPS = 1e-05
F32 = jnp.float32
BF16 = jnp.bfloat16
STEPS = 2
MESH = pl.DeviceIdType.MESH
NT = (((1,), (1,)), ((), ()))

(X_INIT, GAIN, N_ATTN, QKV, O_COL, O_ROW, OUT, X_MID, N_MLP, GU, A_COL, A_ROW, DOWN, X_END) = range(14)


def decode_kernel(dims, h0, h1, cos_ref, sin_ref, lim_ref, gain_ref, wq_h, wk_h, wv_h, wo_h, wg_h, wu_h, wd_h, ck_h, cv_h,
                  out0, out1, kn_ref, vn_ref,
                  wq, wk, wv, wo, wg, wu, wd, ck, cv,
                  xb, x, gains, ns, nb, sbq, rbq, qs, sn, pn, os, ago, no, sbo, rbo, sbg, rbg, aga, na,
                  ssem, rsem, wsem):
    R, C, L, D = dims['R'], dims['C'], dims['L'], dims['D']
    HD = dims['HD']
    SEQ = h0.shape[0] // R
    TOK = SEQ * STEPS
    ALL = TOK * R
    WB = h0.shape[1]
    QC, KC = wq.shape[-1], wk.shape[-1]
    QH, KH = QC // HD, KC // HD
    G = QH // KH
    FF = wg.shape[-1]
    HALVES = R // C
    SLOTS = ck.shape[2]
    r = lax.axis_index('row')
    c = lax.axis_index('col')
    own = c * HALVES

    pairs = [(wq_h, wq), (wk_h, wk), (wv_h, wv), (ck_h, ck), (cv_h, cv), (wo_h, wo), (wg_h, wg), (wu_h, wu), (wd_h, wd)]

    def fetch(layer, i):
        return pltpu.make_async_copy(pairs[i][0].at[layer], pairs[i][1].at[layer], wsem.at[layer, i])

    def wwait(layer, *which):
        for i in which:
            fetch(layer, i).wait()

    for i in range(len(pairs)):
        fetch(0, i).start()

    barrier = pltpu.get_barrier_semaphore()
    for j in range(1, R):
        pl.semaphore_signal(barrier, inc=1, device_id={'row': lax.rem(r + j, R)}, device_id_type=MESH)
    for j in range(1, C):
        pl.semaphore_signal(barrier, inc=1, device_id={'col': lax.rem(c + j, C)}, device_id_type=MESH)

    def row_send(ph, src, dst):
        cps = []
        for j in range(1, R):
            peer = lax.rem(r + j, R)
            cp = pltpu.make_async_remote_copy(src_ref=src(peer), dst_ref=dst(j), send_sem=ssem.at[ph, j - 1],
                                              recv_sem=rsem.at[ph, j - 1], device_id={'row': peer}, device_id_type=MESH)
            cp.start()
            cps.append(cp)
        return cps

    def col_send(ph, src, dst):
        cps = []
        for j in range(1, C):
            peer = lax.rem(c + j, C)
            cp = pltpu.make_async_remote_copy(src_ref=src, dst_ref=dst, send_sem=ssem.at[ph, j - 1],
                                              recv_sem=rsem.at[ph, j - 1], device_id={'col': peer}, device_id_type=MESH)
            cp.start()
            cps.append(cp)
        return cps

    def finish(cps):
        for cp in cps:
            cp.wait_recv()
        for cp in cps:
            cp.wait_send()

    def norm(gi, last):
        ss = jnp.zeros((TOK, 1), F32)
        for k in range(R):
            xk = x[k].astype(F32)
            ss = ss + jnp.sum(xk * xk, axis=-1, keepdims=True)
        scale = lax.rsqrt(ss / D + EPS)
        for k in range(R):
            xk = x[k].astype(F32)
            n = xk * scale * gains[k, pl.ds(gi, 1), :]
            if last is not None:
                n = jnp.where(last, xk, n)
            ns[k] = n.astype(BF16)

    def spread(ph, src, dst):
        cps = row_send(ph, lambda peer: src.at[peer], lambda j: dst.at[r])
        dst[r] = src[r]
        finish(cps)

    for b in range(R):
        xb[b, 0:SEQ] = h0[b * SEQ:(b + 1) * SEQ]
        xb[b, SEQ:TOK] = h1[b * SEQ:(b + 1) * SEQ]
    qs[...] = jnp.zeros_like(qs)
    kn_ref[...] = jnp.zeros_like(kn_ref)
    vn_ref[...] = jnp.zeros_like(vn_ref)
    pl.semaphore_wait(barrier, R + C - 2)
    cps = row_send(X_INIT, lambda peer: xb.at[peer], lambda j: x.at[r])
    cps = cps + row_send(GAIN, lambda peer: gain_ref, lambda j: gains.at[r])
    x[r] = xb[r]
    gains[r] = gain_ref[...]
    finish(cps)
    for layer in range(1, L):
        for i in range(len(pairs)):
            fetch(layer, i).start()
    norm(0, None)
    spread(N_ATTN, ns, nb)

    def layer_body(l, carry):
        wwait(l, 0, 1, 2)
        n = nb[...].reshape(ALL, WB)
        col = 0
        for w, width in ((wq, QC), (wk, KC), (wv, KC)):
            res = jnp.dot(n, w[l], preferred_element_type=F32).astype(BF16)
            sbq[:, :, col:col + width] = res.reshape(R, TOK, width)
            col += width
        cps = row_send(QKV, lambda peer: sbq.at[peer], lambda j: rbq.at[j - 1])
        finish(cps)

        cos = cos_ref[...]
        sin = sin_ref[...]

        def head(i):
            sl = slice(i * HD, (i + 1) * HD)
            a = sbq[r, :, sl].astype(F32)
            for j in range(R - 1):
                a = a + rbq[j, :, sl].astype(F32)
            return a.astype(BF16).astype(F32)

        def rope(v):
            return (v * cos + pltpu.roll(v, HD // 2, 1) * sin).astype(BF16).astype(F32)

        for h in range(QH):
            v = rope(head(h))
            for s in range(STEPS):
                qs[:, s * 8 + h, :] = v[s * SEQ:(s + 1) * SEQ]
        for h in range(KH):
            v = rope(head(QH + h))
            w = head(QH + KH + h)
            for s in range(STEPS):
                kn_ref[l, :, s * KH + h, :] = v[s * SEQ:(s + 1) * SEQ]
                vn_ref[l, :, s * KH + h, :] = w[s * SEQ:(s + 1) * SEQ]

        rows = SEQ * 16
        qall = qs[...].reshape(rows, HD).astype(BF16)
        knew = kn_ref[l].reshape(SEQ * 8, HD).astype(BF16)
        vnew = vn_ref[l].reshape(SEQ * 8, HD).astype(BF16)
        sc = HD ** -0.5
        ri = lax.broadcasted_iota(jnp.int32, (rows, SEQ * 8), 0)
        ci = lax.broadcasted_iota(jnp.int32, (rows, SEQ * 8), 1)
        slot = ci % 8
        kvh = jnp.where(ri % 8 >= G, 1, 0)
        ok = (ri // 16 == ci // 8) & (slot < STEPS * KH) & (slot % KH == kvh) & (slot // KH <= (ri % 16) // 8)
        s_new = lax.dot_general(qall, knew, NT, preferred_element_type=F32) * sc
        sn[...] = jnp.where(ok, s_new, -jnp.inf).reshape(SEQ, 16, SEQ * 8)
        wwait(l, 3, 4)
        kvrow = jnp.where(lax.broadcasted_iota(jnp.int32, (16, SLOTS), 0) % 8 >= G, 1, 0)
        kcol = lax.broadcasted_iota(jnp.int32, (16, SLOTS), 1)
        parity = (kcol % KH) == kvrow

        def attend(b, carry):
            s = lax.dot_general(qs[b].astype(BF16), ck[l, b], NT, preferred_element_type=F32) * sc
            s = jnp.where(parity & (kcol < lim_ref[b]), s, -jnp.inf)
            t = sn[b]
            m = jnp.maximum(jnp.max(s, axis=-1, keepdims=True), jnp.max(t, axis=-1, keepdims=True))
            e = jnp.exp(s - m)
            f = jnp.exp(t - m)
            den = jnp.sum(e, axis=-1, keepdims=True) + jnp.sum(f, axis=-1, keepdims=True)
            pn[b] = (f / den).astype(BF16)
            os[b] = jnp.dot((e / den).astype(BF16), cv[l, b], preferred_element_type=F32)
            return carry

        lax.fori_loop(0, SEQ, attend, 0, unroll=2)
        o_new = jnp.dot(pn[...].reshape(rows, SEQ * 8), vnew, preferred_element_type=F32)
        os[...] = os[...] + o_new.reshape(SEQ, 16, HD)
        per = QH // HALVES
        for h in range(QH):
            for s in range(STEPS):
                ago[own + h // per, s * SEQ:(s + 1) * SEQ, (h % per) * HD:(h % per + 1) * HD] = os[:, s * 8 + h, :].astype(BF16)
        mine = pl.ds(own, HALVES)
        finish(col_send(O_COL, ago.at[mine], ago.at[mine]))
        spread(O_ROW, ago, no)

        def project(act, w, depth):
            lhs = act[...].reshape(ALL, depth)
            for h in range(HALVES):
                res = jnp.dot(lhs, w[l, :, h * WB:(h + 1) * WB], preferred_element_type=F32).astype(BF16)
                sbo[:, h] = res.reshape(R, TOK, WB)

        def residual(ph, ph_col):
            finish(row_send(ph, lambda peer: sbo.at[peer], lambda j: rbo.at[j - 1]))
            for h in range(HALVES):
                a = sbo[r, h].astype(F32)
                for j in range(R - 1):
                    a = a + rbo[j, h].astype(F32)
                x[own + h] = (x[own + h].astype(F32) + a.astype(BF16).astype(F32)).astype(BF16)
            finish(col_send(ph_col, x.at[mine], x.at[mine]))

        wwait(l, 5)
        project(no, wo, WB)
        residual(OUT, X_MID)
        norm(L + l, None)
        spread(N_MLP, ns, nb)

        wwait(l, 6, 7)
        tile = FF // 4

        def gate_up(t, carry):
            off = pl.multiple_of(t * tile, tile)
            n = nb[...].reshape(ALL, WB)
            for k, w in enumerate((wg, wu)):
                res = jnp.dot(n, w[l, :, pl.ds(off, tile)], preferred_element_type=F32).astype(BF16)
                sbg[:, :, pl.ds(off + k * FF, tile)] = res.reshape(R, TOK, tile)
            return carry

        lax.fori_loop(0, 4, gate_up, 0)
        finish(row_send(GU, lambda peer: sbg.at[peer], lambda j: rbg.at[j - 1]))
        at = FF // 8
        half = FF // HALVES

        def act(t, carry):
            off = pl.multiple_of(t * at, at)

            def total(base):
                sl = pl.ds(base + off, at)
                a = sbg[r, :, sl].astype(F32)
                for j in range(R - 1):
                    a = a + rbg[j, :, sl].astype(F32)
                return a.astype(BF16).astype(F32)

            g = total(0)
            u = total(FF)
            per_half = half // at
            aga[own + t // per_half, :, pl.ds(pl.multiple_of((t % per_half) * at, at), at)] = (jax.nn.silu(g) * u).astype(BF16)
            return carry

        lax.fori_loop(0, 8, act, 0)
        finish(col_send(A_COL, aga.at[mine], aga.at[mine]))
        spread(A_ROW, aga, na)
        wwait(l, 8)
        project(na, wd, half)
        residual(DOWN, X_END)
        norm(l + 1, l == L - 1)
        spread(N_ATTN, ns, nb)
        return carry

    lax.fori_loop(0, L, layer_body, 0)
    for b in range(R):
        out0[b * SEQ:(b + 1) * SEQ] = nb[b, 0:SEQ]
        out1[b * SEQ:(b + 1) * SEQ] = nb[b, SEQ:TOK]


def cache_kernel(len_ref, kn_ref, vn_ref, ck_ref, cv_ref, ok_ref, ov_ref):
    b = pl.program_id(1)
    rows = ck_ref.shape[2]
    new = STEPS * 2
    start = 2 * len_ref[b]
    base = pl.multiple_of(jnp.minimum((start // 16) * 16, rows - 32), 16)
    win = pl.ds(base, 32)
    idx = lax.broadcasted_iota(jnp.int32, (32, ck_ref.shape[3]), 0) + base - start
    for src, fresh, dst in ((ck_ref, kn_ref, ok_ref), (cv_ref, vn_ref, ov_ref)):
        dst[...] = src[...]
        val = src[0, 0, win, :].astype(F32)
        for i in range(new):
            val = jnp.where(idx == i, fresh[0, 0, i:i + 1, :], val)
        dst[0, 0, win, :] = val.astype(BF16)


def solution(mesh):
    R, C = mesh.shape['row'], mesh.shape['col']
    hidden_spec = P('rep', 'row')
    index_spec = P(('rep', 'row'))
    cache_spec = P(None, ('rep', 'row'), None, 'col', None)
    gain_spec = P(None, 'row')
    weight_spec = P(None, 'row', 'col')

    def device_program(hidden_0, hidden_1, positions, lengths, cache_k, cache_v, norm_attn, norm_mlp, w_query, w_key, w_value, w_out, w_gate, w_up, w_down):
        L, SEQ, CTX, KH, HD = cache_k.shape
        WB = hidden_0.shape[1]
        TOK = SEQ * STEPS
        QC, KC, FF = w_query.shape[-1], w_key.shape[-1], w_gate.shape[-1]
        HALVES = R // C
        SLOTS = CTX * KH
        inv_freq = jnp.power(jnp.float32(ROPE_BASE), -jnp.arange(HD // 2, dtype=F32) * 2.0 / HD)
        pos = jnp.concatenate([positions + s for s in range(STEPS)])
        angles = pos.astype(F32)[:, None] * inv_freq
        cosine, sine = jnp.cos(angles), jnp.sin(angles)
        cos2 = jnp.concatenate([cosine, cosine], axis=1)
        sin2 = jnp.concatenate([-sine, sine], axis=1)
        lim = jnp.broadcast_to((lengths * KH)[:, None, None], (SEQ, 16, 1))
        gain = jnp.concatenate([norm_attn, norm_mlp, jnp.zeros((8 - 2 * L, WB), BF16)]).astype(F32)
        ck = cache_k.reshape(L, SEQ, SLOTS, HD)
        cv = cache_v.reshape(L, SEQ, SLOTS, HD)
        vm = pl.BlockSpec(memory_space=pltpu.VMEM)
        hbm = pl.BlockSpec(memory_space=pl.ANY)
        weights = (w_query, w_key, w_value, w_out, w_gate, w_up, w_down)
        scratch = [pltpu.VMEM(w.shape, BF16) for w in weights] + [pltpu.VMEM(ck.shape, BF16)] * 2
        scratch += [pltpu.VMEM(s, d) for s, d in (
            ((R, TOK, WB), BF16), ((R, TOK, WB), BF16), ((R, 8, WB), F32), ((R, TOK, WB), BF16), ((R, TOK, WB), BF16),
            ((R, TOK, QC + 2 * KC), BF16), ((R - 1, TOK, QC + 2 * KC), BF16),
            ((SEQ, 16, HD), F32), ((SEQ, 16, SEQ * 8), F32), ((SEQ, 16, SEQ * 8), BF16), ((SEQ, 16, HD), F32),
            ((R, TOK, WB), BF16), ((R, TOK, WB), BF16),
            ((R, HALVES, TOK, WB), BF16), ((R - 1, HALVES, TOK, WB), BF16),
            ((R, TOK, 2 * FF), BF16), ((R - 1, TOK, 2 * FF), BF16),
            ((R, TOK, FF // HALVES), BF16), ((R, TOK, FF // HALVES), BF16))]
        scratch += [pltpu.SemaphoreType.DMA((14, R - 1)), pltpu.SemaphoreType.DMA((14, R - 1)), pltpu.SemaphoreType.DMA((L, 9))]
        dims = dict(R=R, C=C, L=L, D=WB * R, HD=HD)
        out_0, out_1, k_new, v_new = pl.pallas_call(
            functools.partial(decode_kernel, dims),
            out_shape=(jax.ShapeDtypeStruct(hidden_0.shape, BF16), jax.ShapeDtypeStruct(hidden_1.shape, BF16),
                       jax.ShapeDtypeStruct((L, SEQ, 8, HD), F32), jax.ShapeDtypeStruct((L, SEQ, 8, HD), F32)),
            in_specs=[vm] * 6 + [hbm] * 9,
            out_specs=(vm, vm, vm, vm),
            scratch_shapes=scratch,
            compiler_params=pltpu.CompilerParams(collective_id=0, has_side_effects=True, vmem_limit_bytes=62 * 1024 * 1024),
            name='decode',
        )(hidden_0, hidden_1, cos2, sin2, lim, gain, *weights, ck, cv)

        block = pl.BlockSpec((1, 1, SLOTS, HD), lambda l, b, n: (l, b, 0, 0))
        fresh = pl.BlockSpec((1, 1, 8, HD), lambda l, b, n: (l, b, 0, 0))
        ok, ov = pl.pallas_call(
            cache_kernel,
            out_shape=(jax.ShapeDtypeStruct(ck.shape, BF16),) * 2,
            grid_spec=pltpu.PrefetchScalarGridSpec(num_scalar_prefetch=1, grid=(L, SEQ), in_specs=[fresh, fresh, block, block],
                                                   out_specs=(block, block)),
            name='cache_update',
        )(lengths, k_new, v_new, ck, cv)
        return out_0, out_1, ok.reshape(cache_k.shape), ov.reshape(cache_v.shape)

    return jax.shard_map(device_program, mesh=mesh,
                         in_specs=(hidden_spec, hidden_spec, index_spec, index_spec, cache_spec, cache_spec, gain_spec, gain_spec) + (weight_spec,) * 7,
                         out_specs=(hidden_spec, hidden_spec, cache_spec, cache_spec), check_vma=False)
```

time: 966 us -> 257 us (0.27); the launches traced: 955 us -> 256 us
  waiting for transfers between devices: 348 us -> 0 us
  blocking collectives: 329 us -> 0 us
  Pallas kernels: 0 us -> 249 us
  local copies, waits for them, and re-layouts: 97.9 us -> 2.11 us
  starting transfers between devices: 85.3 us -> 0 us
  matrix products: 61.8 us -> 0 us
  between operations: 14.8 us -> 0.66 us
  other arithmetic: 17.9 us -> 4.26 us
    reduce_scatter x16 -> x0, waiting for transfers between devices: 325 us -> none  [sum_rows(): lax.psum_scatter(partial.astype(jnp.bfloat16), 'row', scatter_dimension=0...]
    pallas_call x0 -> x2, Pallas kernels: none -> 249 us  [the longest x1 226 us: device_program(): pl.pallas_call(functools.partial(decode_kernel, dims), out_shape=(jax.Sha...]
    all_gather x16 -> x0, blocking collectives: 156 us -> none  [to_row_features(): whole = lax.all_gather(block, 'col', axis=1, tiled=True)]
    all_to_all x7 -> x0, blocking collectives: 95.5 us -> none  [to_row_features(): return lax.all_to_all(whole, 'row', 1, 0, tiled=True)]
    all_to_all x9 -> x0, starting transfers between devices: 84.1 us -> none  [to_row_features(): return lax.all_to_all(whole, 'row', 1, 0, tiled=True)]
    psum x6 -> x0, blocking collectives: 77.1 us -> none  [rms_norm(): lax.psum(jnp.sum(hidden_f * hidden_f, axis=-1, keepdims=True), 'row')]
    slice x8 -> x0, local copies, waits for them, and re-layouts: 57.7 us -> none  [the longest x4 28.9 us: decoder_layer(): cache_k[layer]]
    dot_general x32 -> x0, matrix products: 46.2 us -> none  [the longest x4 11.9 us: attend_local(): jnp.einsum('bkgl,blkd->bkgd', probs, vals, preferred_element_type=jnp.flo...]
  transfers between devices with their start and end apart: 25 -> 0, of which waited for: 22 -> 0; matrix products, arithmetic and copies ran while one was open for 3% -> 0% of each run, Pallas kernels for 0% -> 0%
where the time goes in v1:
time: 257 us; the launch traced here: 256 us
  Pallas kernels  249 us (97%)
  other arithmetic  4.26 us (2%)
    pallas_call x1, Pallas kernels, device_program(): pl.pallas_call(functools.partial(decode_kernel, dims), out_shape=(jax.Sha...  226 us
    pallas_call x1, Pallas kernels, device_program(): pl.pallas_call(cache_kernel, out_shape=(jax.ShapeDtypeStruct(ck.shape, BF...  23.1 us

profile of v1, /device:TPU:97, one launch (start us, length us, event | category | flops | bytes accessed | tf_op | source)
XLA Modules:
  0.0 256.4 jit_solution(13177922243868482218)
XLA Ops:
  0.6 0.7 broadcast_add_fusion
  1.3 0.7 add_convert_fusion
  2.0 0.7 broadcast_multiply_fusion
  2.7 0.1 pad.2.clone
  2.8 1.4 maximum_convert_fusion.gain_ref
  4.1 0.1 fusion
  4.3 0.7 pad_maximum_fusion
  5.0 0.7 broadcast_in_dim.4.lim_ref
  5.7 226.2 %decode.1 = (bf16[128,384]{1,0:T(8,128)(2,1)}, bf16[128,384]{1,0:T(8,128)(2,1)}, f32[2,16,8,128]{3,2,1,0:T(8,128)}, f32[2,16,8,128]{3,2,1,0:T(8,128)}) custom-call(bf16[128,384]{1,0:T(8,128)(2,1)} %h0.1, bf16[128,384]{1,0:T(8,128)(2,1)} %h1.1, f32[32,128]{1,0:T(8,128)} %get-tuple-element.19.cos_ref, f32[32,128]{1,0:T(8,128)} %get-tuple-element.20.sin_ref, ...), custom_call_target="tpu_custom_call" | custom-call | tf_op jit(solution)/shard_map/decode/pallas_call | solution.py:321
  231.9 0.0 copy-start.1
  231.9 0.0 copy-start
  232.0 23.1 %cache_update.1 = (bf16[2,16,1024,128]{3,2,1,0:T(8,128)(2,1)}, bf16[2,16,1024,128]{3,2,1,0:T(8,128)(2,1)}) custom-call(s32[16]{0:T(128)} %len_ref.1, f32[2,16,8,128]{3,2,1,0:T(8,128)} %get-tuple-element.12.kn_ref, f32[2,16,8,128]{3,2,1,0:T(8,128)} %get-tuple-element.13.vn_ref, bf16[2,16,1024,128]{3,2,1,0:T(8,128)(2,1)} %bitcast.5, ...), custom_call_target="tpu_custom_call" | custom-call | tf_op jit(solution)/shard_map/cache_update/pallas_call | solution.py:334
  255.1 0.0 copy-done.1
  255.1 0.6 copy.21
  255.7 0.0 copy-done
  255.7 0.6 copy.22
  (2 shorter events, 0.0 us)
Async XLA Ops:
  231.9 23.1 %copy-start.1 = (bf16[128,384]{1,0:T(8,128)(2,1)S(1)}, bf16[128,384]{1,0:T(8,128)(2,1)}, u32[]{:S(2)}) copy-start(bf16[128,384]{1,0:T(8,128)(2,1)} %get-tuple-element.25) | copy-start | bytes 294916
  231.9 23.8 %copy-start = (bf16[128,384]{1,0:T(8,128)(2,1)S(1)}, bf16[128,384]{1,0:T(8,128)(2,1)}, u32[]{:S(2)}) copy-start(bf16[128,384]{1,0:T(8,128)(2,1)} %get-tuple-element.26) | copy-start | bytes 294916

commit v2 on v0

v2 whole, which is shorter than its diff:
```python
import functools

import jax
import jax.numpy as jnp
from jax import lax
from jax.experimental import pallas as pl
from jax.experimental.pallas import tpu as pltpu
from jax.sharding import PartitionSpec as P

ROPE_BASE = 1000000.0
EPS = 1e-05
F32 = jnp.float32
BF16 = jnp.bfloat16
STEPS = 2
MESH = pl.DeviceIdType.MESH
NT = (((1,), (1,)), ((), ()))

CORES = 2
COPY_GROUPS = 4
STREAMS = 2

(X_INIT, GAIN, N_ATTN, QKV_A, QKV_B, O_COL, O_ROW, OUT_A, OUT_B, X_MID, N_MLP, GU_A, GU_B, A_COL, A_ROW, DOWN_A, DOWN_B,
 X_END, PHASES) = range(19)
PRE = {QKV_B: QKV_A, GU_B: GU_A, OUT_B: None, DOWN_B: None}


def decode_kernel(dims, h0, h1, cos_ref, sin_ref, lim_ref, gain_ref, wq_h, wk_h, wv_h, wo_h, wg_h, wu_h, wd_h, ck_h, cv_h,
                  out0, out1, kn_ref, vn_ref,
                  wq, wk, wv, wo, wg, wu, wd, ck, cv,
                  xb, x, gains, ns, nb, sbq, prq, rbq, qs, sn, pn, os, ago, no, sbo, pro, rbo, sbg, prg, rbg, aga, na,
                  ssem, rsem, wsem):
    R, C, L, D = dims['R'], dims['C'], dims['L'], dims['D']
    HD = dims['HD']
    SEQ = h0.shape[0] // R
    SZ = SEQ // STREAMS
    TOK = SZ * STEPS
    ALL = TOK * R
    WB = h0.shape[1]
    QC, KC = wq.shape[-1], wk.shape[-1]
    QH, KH = QC // HD, KC // HD
    G = QH // KH
    FF = wg.shape[-1]
    HALVES = R // C
    SLOTS = ck.shape[2]
    XS = R // CORES
    r = lax.axis_index('row')
    c = lax.axis_index('col')
    chip, core = lax.div(r, CORES), lax.rem(r, CORES)
    own = c * HALVES
    mine = pl.ds(own, HALVES)

    pairs = [(wq_h, wq), (wk_h, wk), (wv_h, wv), (ck_h, ck), (cv_h, cv), (wo_h, wo), (wg_h, wg), (wu_h, wu), (wd_h, wd)]

    def fetch(layer, i):
        return pltpu.make_async_copy(pairs[i][0].at[layer], pairs[i][1].at[layer], wsem.at[layer, i])

    def wwait(layer, *which):
        for i in which:
            fetch(layer, i).wait()

    for i in range(len(pairs)):
        fetch(0, i).start()

    barrier = pltpu.get_barrier_semaphore()
    for j in range(1, R):
        pl.semaphore_signal(barrier, inc=1, device_id={'row': lax.rem(r + j, R)}, device_id_type=MESH)
    for j in range(1, C):
        pl.semaphore_signal(barrier, inc=1, device_id={'col': lax.rem(c + j, C)}, device_id_type=MESH)

    def remote(ph, z, j, src, dst, device):
        return pltpu.make_async_remote_copy(src_ref=src, dst_ref=dst, send_sem=ssem.at[ph, z, j], recv_sem=rsem.at[ph, z, j],
                                            device_id=device, device_id_type=MESH)

    def row_copies(ph, z, src, dst):
        for j in range(1, R):
            peer = lax.rem(r + j, R)
            yield remote(ph, z, j - 1, src(peer), dst(j), {'row': peer})

    def chip_copies(ph, z, src, dst):
        for j in range(1, XS):
            peer = lax.rem(chip + j, XS)
            yield remote(ph, z, j - 1, src(peer), dst(j), {'row': peer * CORES + core})

    def col_copies(ph, z, src, dst):
        for j in range(1, C):
            yield remote(ph, z, j - 1, src, dst, {'col': lax.rem(c + j, C)})

    def core_copies(ph, z, src, dst):
        yield remote(ph, z, 0, src, dst, {'row': r + 1 - 2 * core})

    def start(copies):
        for cp in copies:
            cp.start()

    def finish(copies):
        cps = list(copies)
        for cp in cps:
            cp.wait_recv()
        for cp in cps:
            cp.wait_send()

    def spread(ph, z, src, dst):
        return row_copies(ph, z, lambda peer: src.at[z, peer], lambda j: dst.at[z, r])

    def spread_start(ph, z, src, dst):
        start(spread(ph, z, src, dst))
        dst[z, r] = src[z, r]

    def gather(ph, z, buf):
        return col_copies(ph, z, buf.at[z, mine], buf.at[z, mine])

    def core_sum(ph, z, sb, pr):
        return core_copies(ph, z, sb.at[z, 1 - core], pr.at[z])

    def chip_sum(ph, z, sb, rb):
        return chip_copies(ph, z, lambda peer: sb.at[z, core, peer], lambda j: rb.at[z, j - 1])

    def row_sum(ph, z, sb, rb):
        return row_copies(ph, z, lambda peer: sb.at[z, lax.rem(peer, CORES), lax.div(peer, CORES)], lambda j: rb.at[z, j - 1])

    def sum_start(ph, z, sb, pr, rb):
        start(core_sum(PRE[ph], z, sb, pr) if PRE[ph] is not None else row_sum(ph, z, sb, rb))

    def sum_middle(ph, z, sb, pr, rb, tiles):
        if PRE[ph] is None:
            return
        finish(core_sum(PRE[ph], z, sb, pr))
        width = sb.shape[-1] // tiles

        def add(t, carry):
            sl = pl.ds(pl.multiple_of(t * width, width), width)
            sb[z, core, :, :, sl] = (sb[z, core, :, :, sl].astype(F32) + pr[z, :, :, sl].astype(F32)).astype(BF16)
            return carry

        lax.fori_loop(0, tiles, add, 0)
        start(chip_sum(ph, z, sb, rb))

    def sum_finish(ph, z, sb, rb):
        finish(chip_sum(ph, z, sb, rb) if PRE[ph] is not None else row_sum(ph, z, sb, rb))

    def total(ph, z, sb, rb, sl):
        a = sb[z, core, chip, :, sl].astype(F32)
        for j in range((XS if PRE[ph] is not None else R) - 1):
            a = a + rb[z, j, :, sl].astype(F32)
        return a.astype(BF16).astype(F32)

    def put(sb, z, cols, res):
        v = res.astype(BF16).reshape(XS, CORES, TOK, res.shape[-1])
        for k in range(CORES):
            sb[z, k, :, :, cols] = v[:, k]

    def norm(z, gi, last):
        ss = jnp.zeros((TOK, 1), F32)
        for k in range(R):
            xk = x[z, k].astype(F32)
            ss = ss + jnp.sum(xk * xk, axis=-1, keepdims=True)
        scale = lax.rsqrt(ss / D + EPS)
        for k in range(R):
            xk = x[z, k].astype(F32)
            n = xk * scale * gains[k, pl.ds(gi, 1), :]
            if last is not None:
                n = jnp.where(last, xk, n)
            ns[z, k] = n.astype(BF16)

    for b in range(R):
        v0 = h0[b * SEQ:(b + 1) * SEQ].astype(F32)
        v1 = h1[b * SEQ:(b + 1) * SEQ].astype(F32)
        for z in range(STREAMS):
            part = slice(z * SZ, (z + 1) * SZ)
            xb[z, b] = jnp.concatenate([v0[part], v1[part]], axis=0).astype(BF16)
    qs[...] = jnp.zeros_like(qs)
    kn_ref[...] = jnp.zeros_like(kn_ref)
    vn_ref[...] = jnp.zeros_like(vn_ref)
    pl.semaphore_wait(barrier, R + C - 2)

    def gain_copies():
        return row_copies(GAIN, 0, lambda peer: gain_ref, lambda j: gains.at[r])

    for z in range(STREAMS):
        spread_start(X_INIT, z, xb, x)
        if z == 0:
            start(gain_copies())
    gains[r] = gain_ref[...]
    for layer in range(1, L):
        for i in range(len(pairs)):
            fetch(layer, i).start()
    for z in range(STREAMS):
        finish(spread(X_INIT, z, xb, x))
        if z == 0:
            finish(gain_copies())
        norm(z, 0, None)
        spread_start(N_ATTN, z, ns, nb)

    rows = SZ * 16
    sc = HD ** -0.5
    ri = lax.broadcasted_iota(jnp.int32, (rows, SZ * 8), 0)
    ci = lax.broadcasted_iota(jnp.int32, (rows, SZ * 8), 1)
    slot = ci % 8
    kvh = jnp.where(ri % 8 >= G, 1, 0)
    new_ok = (ri // 16 == ci // 8) & (slot < STEPS * KH) & (slot % KH == kvh) & (slot // KH <= (ri % 16) // 8)
    per = QH // HALVES
    tile = FF // 4
    half = FF // HALVES

    def layer_body(l, carry):
        def qkv(z):
            finish(spread(N_ATTN, z, ns, nb))
            if z == 0:
                wwait(l, 0, 1, 2)
            n = nb[z].reshape(ALL, WB)
            col = 0
            for w, width in ((wq, QC), (wk, KC), (wv, KC)):
                put(sbq, z, slice(col, col + width), jnp.dot(n, w[l], preferred_element_type=F32))
                col += width
            sum_start(QKV_B, z, sbq, prq, rbq)

        def qkv_middle(z):
            sum_middle(QKV_B, z, sbq, prq, rbq, 2)

        def attention(z):
            sum_finish(QKV_B, z, sbq, rbq)
            cos = cos_ref[z]
            sin = sin_ref[z]

            def head(i):
                return total(QKV_B, z, sbq, rbq, slice(i * HD, (i + 1) * HD))

            def rope(v):
                return (v * cos + pltpu.roll(v, HD // 2, 1) * sin).astype(BF16).astype(F32)

            seqs = slice(z * SZ, (z + 1) * SZ)
            for h in range(QH):
                v = rope(head(h))
                for s in range(STEPS):
                    qs[:, s * 8 + h, :] = v[s * SZ:(s + 1) * SZ]
            for h in range(KH):
                v = rope(head(QH + h))
                w = head(QH + KH + h)
                for s in range(STEPS):
                    kn_ref[l, seqs, s * KH + h, :] = v[s * SZ:(s + 1) * SZ]
                    vn_ref[l, seqs, s * KH + h, :] = w[s * SZ:(s + 1) * SZ]

            qall = qs[...].reshape(rows, HD).astype(BF16)
            knew = kn_ref[l, seqs].reshape(SZ * 8, HD).astype(BF16)
            vnew = vn_ref[l, seqs].reshape(SZ * 8, HD).astype(BF16)
            s_new = lax.dot_general(qall, knew, NT, preferred_element_type=F32) * sc
            sn[...] = jnp.where(new_ok, s_new, -jnp.inf).reshape(SZ, 16, SZ * 8)
            if z == 0:
                wwait(l, 3, 4)
            kvrow = jnp.where(lax.broadcasted_iota(jnp.int32, (16, SLOTS), 0) % 8 >= G, 1, 0)
            kcol = lax.broadcasted_iota(jnp.int32, (16, SLOTS), 1)
            parity = (kcol % KH) == kvrow

            def attend(b, carry):
                q = z * SZ + b
                s = lax.dot_general(qs[b].astype(BF16), ck[l, q], NT, preferred_element_type=F32) * sc
                s = jnp.where(parity & (kcol < lim_ref[q]), s, -jnp.inf)
                t = sn[b]
                m = jnp.maximum(jnp.max(s, axis=-1, keepdims=True), jnp.max(t, axis=-1, keepdims=True))
                e = jnp.exp(s - m)
                f = jnp.exp(t - m)
                den = jnp.sum(e, axis=-1, keepdims=True) + jnp.sum(f, axis=-1, keepdims=True)
                pn[b] = (f / den).astype(BF16)
                os[b] = jnp.dot((e / den).astype(BF16), cv[l, q], preferred_element_type=F32)
                return carry

            lax.fori_loop(0, SZ, attend, 0, unroll=4)
            o_new = jnp.dot(pn[...].reshape(rows, SZ * 8), vnew, preferred_element_type=F32)
            os[...] = os[...] + o_new.reshape(SZ, 16, HD)
            for h in range(QH):
                o = jnp.concatenate([os[:, s * 8 + h, :] for s in range(STEPS)], axis=0)
                ago[z, own + h // per, :, (h % per) * HD:(h % per + 1) * HD] = o.astype(BF16)
            start(gather(O_COL, z, ago))

        def o_row(z):
            finish(gather(O_COL, z, ago))
            spread_start(O_ROW, z, ago, no)

        def project(act, z, w, depth, ph):
            lhs = act[z].reshape(ALL, depth)
            for h in range(HALVES):
                put(sbo, z, slice(h * WB, (h + 1) * WB),
                    jnp.dot(lhs, w[l, :, h * WB:(h + 1) * WB], preferred_element_type=F32))
            sum_start(ph, z, sbo, pro, rbo)

        def out(z):
            finish(spread(O_ROW, z, ago, no))
            if z == 0:
                wwait(l, 5)
            project(no, z, wo, WB, OUT_B)

        def residual(z, ph, ph_col):
            sum_finish(ph, z, sbo, rbo)
            for h in range(HALVES):
                a = total(ph, z, sbo, rbo, slice(h * WB, (h + 1) * WB))
                x[z, own + h] = (x[z, own + h].astype(F32) + a).astype(BF16)
            start(gather(ph_col, z, x))

        def mlp_norm(z):
            finish(gather(X_MID, z, x))
            norm(z, L + l, None)
            spread_start(N_MLP, z, ns, nb)

        def gate_up(z):
            finish(spread(N_MLP, z, ns, nb))
            if z == 0:
                wwait(l, 6, 7)

            def body(t, carry):
                off = pl.multiple_of(t * tile, tile)
                n = nb[z].reshape(ALL, WB)
                for k, w in enumerate((wg, wu)):
                    put(sbg, z, pl.ds(off + k * FF, tile), jnp.dot(n, w[l, :, pl.ds(off, tile)], preferred_element_type=F32))
                return carry

            lax.fori_loop(0, 4, body, 0)
            sum_start(GU_B, z, sbg, prg, rbg)

        def gate_up_middle(z):
            sum_middle(GU_B, z, sbg, prg, rbg, 8)

        def act(z):
            sum_finish(GU_B, z, sbg, rbg)
            per_half = half // tile

            def body(t, carry):
                off = pl.multiple_of(t * tile, tile)
                g = total(GU_B, z, sbg, rbg, pl.ds(off, tile))
                u = total(GU_B, z, sbg, rbg, pl.ds(off + FF, tile))
                aga[z, own + t // per_half, :, pl.ds(pl.multiple_of((t % per_half) * tile, tile), tile)] = (jax.nn.silu(g) * u).astype(BF16)
                return carry

            lax.fori_loop(0, 4, body, 0)
            start(gather(A_COL, z, aga))

        def a_row(z):
            finish(gather(A_COL, z, aga))
            spread_start(A_ROW, z, aga, na)

        def down(z):
            finish(spread(A_ROW, z, aga, na))
            if z == 0:
                wwait(l, 8)
            project(na, z, wd, half, DOWN_B)

        def end_norm(z):
            finish(gather(X_END, z, x))
            norm(z, l + 1, l == L - 1)
            spread_start(N_ATTN, z, ns, nb)

        stages = [qkv, qkv_middle, attention, o_row, out]
        stages += [lambda z: sum_middle(OUT_B, z, sbo, pro, rbo, 1)] if PRE[OUT_B] is not None else []
        stages += [lambda z: residual(z, OUT_B, X_MID), mlp_norm, gate_up, gate_up_middle, act, a_row, down]
        stages += [lambda z: sum_middle(DOWN_B, z, sbo, pro, rbo, 1)] if PRE[DOWN_B] is not None else []
        stages += [lambda z: residual(z, DOWN_B, X_END), end_norm]
        for stage in stages:
            for z in range(STREAMS):
                stage(z)
        return carry

    lax.fori_loop(0, L, layer_body, 0)
    for z in range(STREAMS):
        finish(spread(N_ATTN, z, ns, nb))
    for b in range(R):
        v = [nb[z, b].astype(F32) for z in range(STREAMS)]
        for s, out in enumerate((out0, out1)):
            out[b * SEQ:(b + 1) * SEQ] = jnp.concatenate([w[s * SZ:(s + 1) * SZ] for w in v], axis=0).astype(BF16)


def cache_kernel(heads, len_ref, kn_ref, vn_ref, ck_ref, cv_ref, ok_ref, ov_ref, kbuf, vbuf, rsem, wsem):
    layers, seqs, rows, width = ck_ref.shape
    group = seqs // COPY_GROUPS
    sides = ((ck_ref, kbuf, kn_ref, ok_ref), (cv_ref, vbuf, vn_ref, ov_ref))

    def load(k, i):
        at = (i // COPY_GROUPS, pl.ds((i % COPY_GROUPS) * group, group))
        return pltpu.make_async_copy(sides[k][0].at[at], sides[k][1].at[i], rsem.at[k, i])

    def save(k, i):
        at = (i // COPY_GROUPS, pl.ds((i % COPY_GROUPS) * group, group))
        return pltpu.make_async_copy(sides[k][1].at[i], sides[k][3].at[at], wsem.at[k, i])

    count = layers * COPY_GROUPS
    for i in range(count):
        for k in range(2):
            load(k, i).start()
    for i in range(count):
        layer, first = i // COPY_GROUPS, (i % COPY_GROUPS) * group
        for k in range(2):
            load(k, i).wait()

            def patch(g, carry):
                buf, fresh = sides[k][1], sides[k][2]
                at = len_ref[first + g] * heads
                base = pl.multiple_of(jnp.minimum((at // 16) * 16, rows - 32), 16)
                win = pl.ds(base, 32)
                idx = lax.broadcasted_iota(jnp.int32, (32, width), 0) + base - at
                val = buf[i, g, win, :].astype(F32)
                new = fresh[layer, first + g]
                for n in range(STEPS * heads):
                    val = jnp.where(idx == n, new[n:n + 1, :], val)
                buf[i, g, win, :] = val.astype(BF16)
                return carry

            lax.fori_loop(0, group, patch, 0, unroll=True)
            save(k, i).start()
    for i in range(count):
        for k in range(2):
            save(k, i).wait()


def solution(mesh):
    R, C = mesh.shape['row'], mesh.shape['col']
    hidden_spec = P('rep', 'row')
    index_spec = P(('rep', 'row'))
    cache_spec = P(None, ('rep', 'row'), None, 'col', None)
    gain_spec = P(None, 'row')
    weight_spec = P(None, 'row', 'col')

    def device_program(hidden_0, hidden_1, positions, lengths, cache_k, cache_v, norm_attn, norm_mlp, w_query, w_key, w_value, w_out, w_gate, w_up, w_down):
        L, SEQ, CTX, KH, HD = cache_k.shape
        WB = hidden_0.shape[1]
        SZ = SEQ // STREAMS
        TOK = SZ * STEPS
        XS = R // CORES
        Z = STREAMS
        QC, KC, FF = w_query.shape[-1], w_key.shape[-1], w_gate.shape[-1]
        HALVES = R // C
        SLOTS = CTX * KH
        inv_freq = jnp.power(jnp.float32(ROPE_BASE), -jnp.arange(HD // 2, dtype=F32) * 2.0 / HD)
        pos = jnp.concatenate([(positions + s).reshape(Z, SZ) for s in range(STEPS)], axis=1)
        angles = pos.astype(F32)[:, :, None] * inv_freq
        cosine, sine = jnp.cos(angles), jnp.sin(angles)
        cos2 = jnp.concatenate([cosine, cosine], axis=2)
        sin2 = jnp.concatenate([-sine, sine], axis=2)
        lim = jnp.broadcast_to((lengths * KH)[:, None, None], (SEQ, 16, 1))
        gain = jnp.concatenate([norm_attn, norm_mlp, jnp.zeros((8 - 2 * L, WB), BF16)]).astype(F32)
        ck = cache_k.reshape(L, SEQ, SLOTS, HD)
        cv = cache_v.reshape(L, SEQ, SLOTS, HD)
        vm = pl.BlockSpec(memory_space=pltpu.VMEM)
        hbm = pl.BlockSpec(memory_space=pl.ANY)
        weights = (w_query, w_key, w_value, w_out, w_gate, w_up, w_down)
        scratch = [pltpu.VMEM(w.shape, BF16) for w in weights] + [pltpu.VMEM(ck.shape, BF16)] * 2
        N3 = QC + 2 * KC
        N2 = 2 * FF
        OUTW = HALVES * WB

        def slots(ph):
            return R - 1 if PRE[ph] is None else XS - 1

        scratch += [pltpu.VMEM(s, d) for s, d in (
            ((Z, R, TOK, WB), BF16), ((Z, R, TOK, WB), BF16), ((R, 8, WB), F32), ((Z, R, TOK, WB), BF16), ((Z, R, TOK, WB), BF16),
            ((Z, CORES, XS, TOK, N3), BF16), ((Z, XS, TOK, N3), BF16), ((Z, slots(QKV_B), TOK, N3), BF16),
            ((SZ, 16, HD), F32), ((SZ, 16, SZ * 8), F32), ((SZ, 16, SZ * 8), BF16), ((SZ, 16, HD), F32),
            ((Z, R, TOK, WB), BF16), ((Z, R, TOK, WB), BF16),
            ((Z, CORES, XS, TOK, OUTW), BF16), ((Z, XS, TOK, OUTW), BF16), ((Z, slots(OUT_B), TOK, OUTW), BF16),
            ((Z, CORES, XS, TOK, N2), BF16), ((Z, XS, TOK, N2), BF16), ((Z, slots(GU_B), TOK, N2), BF16),
            ((Z, R, TOK, FF // HALVES), BF16), ((Z, R, TOK, FF // HALVES), BF16))]
        scratch += [pltpu.SemaphoreType.DMA((PHASES, Z, R - 1))] * 2 + [pltpu.SemaphoreType.DMA((L, 9))]
        dims = dict(R=R, C=C, L=L, D=WB * R, HD=HD)
        out_0, out_1, k_new, v_new = pl.pallas_call(
            functools.partial(decode_kernel, dims),
            out_shape=(jax.ShapeDtypeStruct(hidden_0.shape, BF16), jax.ShapeDtypeStruct(hidden_1.shape, BF16),
                       jax.ShapeDtypeStruct((L, SEQ, 8, HD), F32), jax.ShapeDtypeStruct((L, SEQ, 8, HD), F32)),
            in_specs=[vm] * 6 + [hbm] * 9,
            out_specs=(vm, vm, vm, vm),
            scratch_shapes=scratch,
            compiler_params=pltpu.CompilerParams(collective_id=0, has_side_effects=True, vmem_limit_bytes=62 * 1024 * 1024),
            name='decode',
        )(hidden_0, hidden_1, cos2, sin2, lim, gain, *weights, ck, cv)

        smem = pl.BlockSpec(memory_space=pltpu.SMEM)
        count = L * COPY_GROUPS
        buf = pltpu.VMEM((count, SEQ // COPY_GROUPS, SLOTS, HD), BF16)
        ok, ov = pl.pallas_call(
            functools.partial(cache_kernel, KH),
            out_shape=(jax.ShapeDtypeStruct(ck.shape, BF16),) * 2,
            in_specs=[smem, vm, vm, hbm, hbm],
            out_specs=(hbm, hbm),
            scratch_shapes=[buf, buf, pltpu.SemaphoreType.DMA((2, count)), pltpu.SemaphoreType.DMA((2, count))],
            compiler_params=pltpu.CompilerParams(vmem_limit_bytes=32 * 1024 * 1024),
            name='cache_update',
        )(lengths, k_new, v_new, ck, cv)
        ok, ov = ok.reshape(cache_k.shape), ov.reshape(cache_v.shape)
        return out_0, out_1, ok, ov

    return jax.shard_map(device_program, mesh=mesh,
                         in_specs=(hidden_spec, hidden_spec, index_spec, index_spec, cache_spec, cache_spec, gain_spec, gain_spec) + (weight_spec,) * 7,
                         out_specs=(hidden_spec, hidden_spec, cache_spec, cache_spec), check_vma=False)
```

time: 966 us -> 193 us (0.20); the launches traced: 955 us -> 193 us
  waiting for transfers between devices: 348 us -> 0 us
  blocking collectives: 329 us -> 0 us
  Pallas kernels: 0 us -> 177 us
  local copies, waits for them, and re-layouts: 97.9 us -> 11.5 us
  starting transfers between devices: 85.3 us -> 0 us
  matrix products: 61.8 us -> 0 us
  other arithmetic: 17.9 us -> 3.61 us
  between operations: 14.8 us -> 0.68 us
    reduce_scatter x16 -> x0, waiting for transfers between devices: 325 us -> none  [sum_rows(): lax.psum_scatter(partial.astype(jnp.bfloat16), 'row', scatter_dimension=0...]
    pallas_call x0 -> x2, Pallas kernels: none -> 177 us  [the longest x1 169 us: device_program(): pl.pallas_call(functools.partial(decode_kernel, dims), out_shape=(jax.Sha...]
    all_gather x16 -> x0, blocking collectives: 156 us -> none  [to_row_features(): whole = lax.all_gather(block, 'col', axis=1, tiled=True)]
    all_to_all x7 -> x0, blocking collectives: 95.5 us -> none  [to_row_features(): return lax.all_to_all(whole, 'row', 1, 0, tiled=True)]
    all_to_all x9 -> x0, starting transfers between devices: 84.1 us -> none  [to_row_features(): return lax.all_to_all(whole, 'row', 1, 0, tiled=True)]
    psum x6 -> x0, blocking collectives: 77.1 us -> none  [rms_norm(): lax.psum(jnp.sum(hidden_f * hidden_f, axis=-1, keepdims=True), 'row')]
    slice x8 -> x0, local copies, waits for them, and re-layouts: 57.7 us -> none  [the longest x4 28.9 us: decoder_layer(): cache_k[layer]]
    dot_general x32 -> x0, matrix products: 46.2 us -> none  [the longest x4 11.9 us: attend_local(): jnp.einsum('bkgl,blkd->bkgd', probs, vals, preferred_element_type=jnp.flo...]
  transfers between devices with their start and end apart: 25 -> 0, of which waited for: 22 -> 0; matrix products, arithmetic and copies ran while one was open for 3% -> 0% of each run, Pallas kernels for 0% -> 0%
where the time goes in v2:
time: 193 us
  Pallas kernels  177 us (92%)
  local copies, waits for them, and re-layouts  11.5 us (6%)
  other arithmetic  3.61 us (2%)
    pallas_call x1, Pallas kernels, device_program(): pl.pallas_call(functools.partial(decode_kernel, dims), out_shape=(jax.Sha...  169 us
    unnamed x16, local copies, waits for them, and re-layouts  9.86 us
    pallas_call x1, Pallas kernels, device_program(): pl.pallas_call(functools.partial(cache_kernel, KH), out_shape=(jax.ShapeD...  7.81 us

profile of v2, /device:TPU:97, one launch (start us, length us, event | category | flops | bytes accessed | tf_op | source)
XLA Modules:
  0.0 193.0 jit_solution(3951176834249824386)
XLA Ops:
  0.6 0.7 broadcast_add_fusion
  1.3 0.1 concatenate.21
  1.4 0.7 broadcast_multiply_fusion
  2.0 0.1 pad.2.clone
  2.1 0.7 concatenate.20
  2.9 0.1 add_convert_fusion
  2.9 1.4 maximum_convert_fusion.gain_ref
  4.3 0.1 fusion
  4.5 0.7 pad_maximum_fusion
  5.1 0.7 broadcast_in_dim.4.lim_ref
  5.9 0.0 copy-start.4
  5.9 169.4 %decode.1 = (bf16[128,384]{1,0:T(8,128)(2,1)}, bf16[128,384]{1,0:T(8,128)(2,1)}, f32[2,16,8,128]{3,2,1,0:T(8,128)}, f32[2,16,8,128]{3,2,1,0:T(8,128)}) custom-call(bf16[128,384]{1,0:T(8,128)(2,1)} %h0.1, bf16[128,384]{1,0:T(8,128)(2,1)} %h1.1, f32[2,16,128]{2,1,0:T(8,128)} %get-tuple-element.19.cos_ref, f32[2,16,128]{2,1,0:T(8,128)} %get-tuple-element.20.sin_ref, ...), custom_call_target="tpu_custom_call" | custom-call | tf_op jit(solution)/shard_map/decode/pallas_call | solution.py:461
  175.3 0.0 copy-done.4
  175.3 0.0 copy-start
  175.4 3.4 %copy-done = bf16[2,16,512,2,128]{4,3,2,1,0:T(2,128)(2,1)S(1)} copy-done((bf16[2,16,512,2,128]{4,3,2,1,0:T(2,128)(2,1)S(1)}, bf16[2,16,512,2,128]{4,3,2,1,0:T(2,128)(2,1)}, u32[]{:S(2)}) %copy-start) | copy-done | bytes 8388632
  178.7 0.0 copy-start.1
  178.7 3.4 %copy-done.1 = bf16[2,16,512,2,128]{4,3,2,1,0:T(2,128)(2,1)S(1)} copy-done((bf16[2,16,512,2,128]{4,3,2,1,0:T(2,128)(2,1)S(1)}, bf16[2,16,512,2,128]{4,3,2,1,0:T(2,128)(2,1)}, u32[]{:S(2)}) %copy-start.1) | copy-done | bytes 8388632
  182.1 0.9 copy-done.2
  183.0 0.9 copy-done.3
  183.9 7.8 %cache_update.1 = (bf16[2,16,1024,128]{3,2,1,0:T(8,128)(2,1)}, bf16[2,16,1024,128]{3,2,1,0:T(8,128)(2,1)}) custom-call(s32[16]{0:T(128)S(1)} %copy-done.4, f32[2,16,8,128]{3,2,1,0:T(8,128)S(1)} %copy-done.2, f32[2,16,8,128]{3,2,1,0:T(8,128)S(1)} %copy-done.3, bf16[2,16,1024,128]{3,2,1,0:T(8,128)(2,1)S(1)} %bitcast.5, bf16[2,16,1024,128]{3,2,1,0:T(8,128)(2,1)S(1)} %bitcast.7), custom_call_target="tpu_custom_call" | custom-call | tf_op jit(solution)/shard_map/cache_update/pallas_call | solution.py:475
  191.7 0.0 copy-done.6
  191.8 0.6 copy.21
  192.4 0.0 copy-done.5
  192.4 0.6 copy.22
  (6 shorter events, 0.0 us)
Async XLA Ops:
  5.9 169.4 %copy-start.4 = (s32[16]{0:T(128)S(1)}, s32[16]{0:T(128)}, u32[]{:S(2)}) copy-start(s32[16]{0:T(128)} %len_ref.1) | copy-start | bytes 196
  175.3 3.4 %copy-start = (bf16[2,16,512,2,128]{4,3,2,1,0:T(2,128)(2,1)S(1)}, bf16[2,16,512,2,128]{4,3,2,1,0:T(2,128)(2,1)}, u32[]{:S(2)}) copy-start(bf16[2,16,512,2,128]{4,3,2,1,0:T(2,128)(2,1)} %param.19) | copy-start | bytes 25165828
  178.7 3.4 %copy-start.1 = (bf16[2,16,512,2,128]{4,3,2,1,0:T(2,128)(2,1)S(1)}, bf16[2,16,512,2,128]{4,3,2,1,0:T(2,128)(2,1)}, u32[]{:S(2)}) copy-start(bf16[2,16,512,2,128]{4,3,2,1,0:T(2,128)(2,1)} %param.20) | copy-start | bytes 25165828
  182.1 0.9 copy-start.2
  183.0 0.9 copy-start.3
  183.9 7.8 %copy-start.6 = (bf16[128,384]{1,0:T(8,128)(2,1)S(1)}, bf16[128,384]{1,0:T(8,128)(2,1)}, u32[]{:S(2)}) copy-start(bf16[128,384]{1,0:T(8,128)(2,1)} %get-tuple-element.25) | copy-start | bytes 294916
  183.9 8.5 %copy-start.5 = (bf16[128,384]{1,0:T(8,128)(2,1)S(1)}, bf16[128,384]{1,0:T(8,128)(2,1)}, u32[]{:S(2)}) copy-start(bf16[128,384]{1,0:T(8,128)(2,1)} %get-tuple-element.26) | copy-start | bytes 294916

commit v3 on v2

--- a/solution.py
+++ b/solution.py
@@ -1,4 +1,5 @@
 import functools
+import math
 
 import jax
 import jax.numpy as jnp
@@ -21,13 +22,13 @@
 
 (X_INIT, GAIN, N_ATTN, QKV_A, QKV_B, O_COL, O_ROW, OUT_A, OUT_B, X_MID, N_MLP, GU_A, GU_B, A_COL, A_ROW, DOWN_A, DOWN_B,
  X_END, PHASES) = range(19)
-PRE = {QKV_B: QKV_A, GU_B: GU_A, OUT_B: None, DOWN_B: None}
-
-
-def decode_kernel(dims, h0, h1, cos_ref, sin_ref, lim_ref, gain_ref, wq_h, wk_h, wv_h, wo_h, wg_h, wu_h, wd_h, ck_h, cv_h,
+PRE = {QKV_B: None, GU_B: GU_A, OUT_B: None, DOWN_B: None}
+
+
+def decode_kernel(dims, h0, h1, pos_ref, len_ref, ga_ref, gm_ref, wq_h, wk_h, wv_h, wo_h, wg_h, wu_h, wd_h, ck_h, cv_h,
                   out0, out1, kn_ref, vn_ref,
                   wq, wk, wv, wo, wg, wu, wd, ck, cv,
-                  xb, x, gains, ns, nb, sbq, prq, rbq, qs, sn, pn, os, ago, no, sbo, pro, rbo, sbg, prg, rbg, aga, na,
+                  cos_ref, sin_ref, gain_ref, xb, x, gains, ns, nb, sbq, prq, rbq, qs, sn, pn, os, ago, no, sbo, pro, rbo, sbg, prg, rbg, aga, na,
                   ssem, rsem, wsem):
     R, C, L, D = dims['R'], dims['C'], dims['L'], dims['D']
     HD = dims['HD']
@@ -162,6 +163,22 @@
                 n = jnp.where(last, xk, n)
             ns[z, k] = n.astype(BF16)
 
+    gain_ref[...] = jnp.zeros_like(gain_ref)
+    gain_ref[0:L] = ga_ref[...].astype(F32)
+    gain_ref[L:2 * L] = gm_ref[...].astype(F32)
+    lane = lax.broadcasted_iota(jnp.int32, (TOK, HD), 1)
+    token = lax.broadcasted_iota(jnp.int32, (TOK, HD), 0)
+    half_lane = lax.rem(lane, HD // 2)
+    inv_freq = jnp.exp(half_lane.astype(F32) * (-2.0 / HD * math.log(ROPE_BASE)))
+    for z in range(STREAMS):
+        position = jnp.zeros((TOK, HD), jnp.int32)
+        for b in range(SZ):
+            position = jnp.where(lax.rem(token, SZ) == b, pos_ref[z * SZ + b], position)
+        angle = (position + lax.div(token, SZ)).astype(F32) * inv_freq
+        cos_ref[z] = jnp.cos(angle)
+        sine = jnp.sin(angle)
+        sin_ref[z] = jnp.where(lane < HD // 2, -sine, sine)
+
     for b in range(R):
         v0 = h0[b * SEQ:(b + 1) * SEQ].astype(F32)
         v1 = h1[b * SEQ:(b + 1) * SEQ].astype(F32)
@@ -254,7 +271,7 @@
             def attend(b, carry):
                 q = z * SZ + b
                 s = lax.dot_general(qs[b].astype(BF16), ck[l, q], NT, preferred_element_type=F32) * sc
-                s = jnp.where(parity & (kcol < lim_ref[q]), s, -jnp.inf)
+                s = jnp.where(parity & (kcol < len_ref[q] * KH), s, -jnp.inf)
                 t = sn[b]
                 m = jnp.maximum(jnp.max(s, axis=-1, keepdims=True), jnp.max(t, axis=-1, keepdims=True))
                 e = jnp.exp(s - m)
@@ -367,10 +384,13 @@
             out[b * SEQ:(b + 1) * SEQ] = jnp.concatenate([w[s * SZ:(s + 1) * SZ] for w in v], axis=0).astype(BF16)
 
 
-def cache_kernel(heads, len_ref, kn_ref, vn_ref, ck_ref, cv_ref, ok_ref, ov_ref, kbuf, vbuf, rsem, wsem):
+def cache_kernel(heads, len_ref, kn_h, vn_h, ck_ref, cv_ref, a0, a1, ok_ref, ov_ref, o0, o1,
+                 kn_ref, vn_ref, kbuf, vbuf, b0, b1, rsem, wsem, nsem):
     layers, seqs, rows, width = ck_ref.shape
     group = seqs // COPY_GROUPS
     sides = ((ck_ref, kbuf, kn_ref, ok_ref), (cv_ref, vbuf, vn_ref, ov_ref))
+    small = [pltpu.make_async_copy(a, b, nsem.at[i]) for i, (a, b) in enumerate(((kn_h, kn_ref), (vn_h, vn_ref), (a0, b0), (a1, b1)))]
+    pass_on = [pltpu.make_async_copy(a, b, nsem.at[4 + i]) for i, (a, b) in enumerate(((b0, o0), (b1, o1)))]
 
     def load(k, i):
         at = (i // COPY_GROUPS, pl.ds((i % COPY_GROUPS) * group, group))
@@ -381,9 +401,15 @@
         return pltpu.make_async_copy(sides[k][1].at[i], sides[k][3].at[at], wsem.at[k, i])
 
     count = layers * COPY_GROUPS
+    for cp in small:
+        cp.start()
     for i in range(count):
         for k in range(2):
             load(k, i).start()
+    for cp in small:
+        cp.wait()
+    for cp in pass_on:
+        cp.start()
     for i in range(count):
         layer, first = i // COPY_GROUPS, (i % COPY_GROUPS) * group
         for k in range(2):
@@ -404,6 +430,8 @@
 
             lax.fori_loop(0, group, patch, 0, unroll=True)
             save(k, i).start()
+    for cp in pass_on:
+        cp.wait()
     for i in range(count):
         for k in range(2):
             save(k, i).wait()
@@ -427,17 +455,10 @@
         QC, KC, FF = w_query.shape[-1], w_key.shape[-1], w_gate.shape[-1]
         HALVES = R // C
         SLOTS = CTX * KH
-        inv_freq = jnp.power(jnp.float32(ROPE_BASE), -jnp.arange(HD // 2, dtype=F32) * 2.0 / HD)
-        pos = jnp.concatenate([(positions + s).reshape(Z, SZ) for s in range(STEPS)], axis=1)
-        angles = pos.astype(F32)[:, :, None] * inv_freq
-        cosine, sine = jnp.cos(angles), jnp.sin(angles)
-        cos2 = jnp.concatenate([cosine, cosine], axis=2)
-        sin2 = jnp.concatenate([-sine, sine], axis=2)
-        lim = jnp.broadcast_to((lengths * KH)[:, None, None], (SEQ, 16, 1))
-        gain = jnp.concatenate([norm_attn, norm_mlp, jnp.zeros((8 - 2 * L, WB), BF16)]).astype(F32)
         ck = cache_k.reshape(L, SEQ, SLOTS, HD)
         cv = cache_v.reshape(L, SEQ, SLOTS, HD)
         vm = pl.BlockSpec(memory_space=pltpu.VMEM)
+        smem = pl.BlockSpec(memory_space=pltpu.SMEM)
         hbm = pl.BlockSpec(memory_space=pl.ANY)
         weights = (w_query, w_key, w_value, w_out, w_gate, w_up, w_down)
         scratch = [pltpu.VMEM(w.shape, BF16) for w in weights] + [pltpu.VMEM(ck.shape, BF16)] * 2
@@ -449,6 +470,7 @@
             return R - 1 if PRE[ph] is None else XS - 1
 
         scratch += [pltpu.VMEM(s, d) for s, d in (
+            ((Z, TOK, HD), F32), ((Z, TOK, HD), F32), ((8, WB), F32),
             ((Z, R, TOK, WB), BF16), ((Z, R, TOK, WB), BF16), ((R, 8, WB), F32), ((Z, R, TOK, WB), BF16), ((Z, R, TOK, WB), BF16),
             ((Z, CORES, XS, TOK, N3), BF16), ((Z, XS, TOK, N3), BF16), ((Z, slots(QKV_B), TOK, N3), BF16),
             ((SZ, 16, HD), F32), ((SZ, 16, SZ * 8), F32), ((SZ, 16, SZ * 8), BF16), ((SZ, 16, HD), F32),
@@ -462,25 +484,27 @@
             functools.partial(decode_kernel, dims),
             out_shape=(jax.ShapeDtypeStruct(hidden_0.shape, BF16), jax.ShapeDtypeStruct(hidden_1.shape, BF16),
                        jax.ShapeDtypeStruct((L, SEQ, 8, HD), F32), jax.ShapeDtypeStruct((L, SEQ, 8, HD), F32)),
-            in_specs=[vm] * 6 + [hbm] * 9,
+            in_specs=[vm, vm, smem, smem, vm, vm] + [hbm] * 9,
             out_specs=(vm, vm, vm, vm),
             scratch_shapes=scratch,
             compiler_params=pltpu.CompilerParams(collective_id=0, has_side_effects=True, vmem_limit_bytes=62 * 1024 * 1024),
             name='decode',
-        )(hidden_0, hidden_1, cos2, sin2, lim, gain, *weights, ck, cv)
-
-        smem = pl.BlockSpec(memory_space=pltpu.SMEM)
+        )(hidden_0, hidden_1, positions, lengths, norm_attn, norm_mlp, *weights, ck, cv)
+
         count = L * COPY_GROUPS
         buf = pltpu.VMEM((count, SEQ // COPY_GROUPS, SLOTS, HD), BF16)
-        ok, ov = pl.pallas_call(
+        fresh = pltpu.VMEM(k_new.shape, F32)
+        hidden = pltpu.VMEM(hidden_0.shape, BF16)
+        ok, ov, out_0, out_1 = pl.pallas_call(
             functools.partial(cache_kernel, KH),
-            out_shape=(jax.ShapeDtypeStruct(ck.shape, BF16),) * 2,
-            in_specs=[smem, vm, vm, hbm, hbm],
-            out_specs=(hbm, hbm),
-            scratch_shapes=[buf, buf, pltpu.SemaphoreType.DMA((2, count)), pltpu.SemaphoreType.DMA((2, count))],
-            compiler_params=pltpu.CompilerParams(vmem_limit_bytes=32 * 1024 * 1024),
+            out_shape=(jax.ShapeDtypeStruct(ck.shape, BF16),) * 2 + (jax.ShapeDtypeStruct(hidden_0.shape, BF16),) * 2,
+            in_specs=[smem] + [hbm] * 6,
+            out_specs=(hbm,) * 4,
+            scratch_shapes=[fresh, fresh, buf, buf, hidden, hidden, pltpu.SemaphoreType.DMA((2, count)),
+                            pltpu.SemaphoreType.DMA((2, count)), pltpu.SemaphoreType.DMA((6,))],
+            compiler_params=pltpu.CompilerParams(vmem_limit_bytes=62 * 1024 * 1024),
             name='cache_update',
-        )(lengths, k_new, v_new, ck, cv)
+        )(lengths, k_new, v_new, ck, cv, out_0, out_1)
         ok, ov = ok.reshape(cache_k.shape), ov.reshape(cache_v.shape)
         return out_0, out_1, ok, ov
 

time: 193 us -> 182 us (0.943)
  local copies, waits for them, and re-layouts: 11.5 us -> 0 us
  Pallas kernels: 177 us -> 181 us
  other arithmetic: 3.61 us -> 0 us
    unnamed x16 -> x0, local copies, waits for them, and re-layouts: 9.86 us -> none
    pallas_call x1, Pallas kernels: 7.81 us -> 12.4 us  [device_program(): pl.pallas_call(functools.partial(cache_kernel, KH), out_shape=(jax.ShapeD...]
where the time goes in v3:
time: 182 us; the launch traced here: 181 us
  Pallas kernels  181 us (99%)
    pallas_call x1, Pallas kernels, device_program(): pl.pallas_call(functools.partial(decode_kernel, dims), out_shape=(jax.Sha...  168 us
    pallas_call x1, Pallas kernels, device_program(): pl.pallas_call(functools.partial(cache_kernel, KH), out_shape=(jax.ShapeD...  12.4 us

profile of v3, /device:TPU:97, one launch (start us, length us, event | category | flops | bytes accessed | tf_op | source)
XLA Modules:
  0.0 181.4 jit_solution(13326383743224270779)
XLA Ops:
  0.6 168.3 %decode.1 = (bf16[128,384]{1,0:T(8,128)(2,1)}, bf16[128,384]{1,0:T(8,128)(2,1)}, f32[2,16,8,128]{3,2,1,0:T(8,128)}, f32[2,16,8,128]{3,2,1,0:T(8,128)}) custom-call(bf16[128,384]{1,0:T(8,128)(2,1)} %h0.1, bf16[128,384]{1,0:T(8,128)(2,1)} %h1.1, s32[16]{0:T(128)} %pos_ref.1, s32[16]{0:T(128)} %len_ref.3, bf16[2,384]{1,0:T(2,128)(2,1)} %ga_ref.1, ...), custom_call_target="tpu_custom_call" | custom-call | tf_op jit(solution)/shard_map/decode/pallas_call | solution.py:483
  169.0 12.4 %cache_update.1 = (bf16[2,16,1024,128]{3,2,1,0:T(8,128)(2,1)}, bf16[2,16,1024,128]{3,2,1,0:T(8,128)(2,1)}, bf16[128,384]{1,0:T(8,128)(2,1)}, bf16[128,384]{1,0:T(8,128)(2,1)}) custom-call(s32[16]{0:T(128)} %len_ref.3, f32[2,16,8,128]{3,2,1,0:T(8,128)} %get-tuple-element.12.kn_h, f32[2,16,8,128]{3,2,1,0:T(8,128)} %get-tuple-element.13.vn_h, ...), custom_call_target="tpu_custom_call" | custom-call | tf_op jit(solution)/shard_map/cache_update/pallas_call | solution.py:498

commit v4 on v3

--- a/solution.py
+++ b/solution.py
@@ -18,7 +18,7 @@
 
 CORES = 2
 COPY_GROUPS = 4
-STREAMS = 2
+STREAMS = 4
 
 (X_INIT, GAIN, N_ATTN, QKV_A, QKV_B, O_COL, O_ROW, OUT_A, OUT_B, X_MID, N_MLP, GU_A, GU_B, A_COL, A_ROW, DOWN_A, DOWN_B,
  X_END, PHASES) = range(19)
@@ -68,64 +68,43 @@
     for j in range(1, C):
         pl.semaphore_signal(barrier, inc=1, device_id={'col': lax.rem(c + j, C)}, device_id_type=MESH)
 
-    def remote(ph, z, j, src, dst, device):
-        return pltpu.make_async_remote_copy(src_ref=src, dst_ref=dst, send_sem=ssem.at[ph, z, j], recv_sem=rsem.at[ph, z, j],
-                                            device_id=device, device_id_type=MESH)
-
-    def row_copies(ph, z, src, dst):
+    def remote(ph, z, src, dst, device):
+        pltpu.make_async_remote_copy(src_ref=src, dst_ref=dst, send_sem=ssem.at[ph, z], recv_sem=rsem.at[ph, z],
+                                     device_id=device, device_id_type=MESH).start()
+
+    def finish(ph, z, received):
+        pltpu.make_async_copy(received, received, rsem.at[ph, z]).wait()
+        pltpu.make_async_copy(received, received, ssem.at[ph, z]).wait()
+
+    def row_send(ph, z, src, dst):
         for j in range(1, R):
             peer = lax.rem(r + j, R)
-            yield remote(ph, z, j - 1, src(peer), dst(j), {'row': peer})
-
-    def chip_copies(ph, z, src, dst):
-        for j in range(1, XS):
-            peer = lax.rem(chip + j, XS)
-            yield remote(ph, z, j - 1, src(peer), dst(j), {'row': peer * CORES + core})
-
-    def col_copies(ph, z, src, dst):
+            remote(ph, z, src(peer), dst(j), {'row': peer})
+
+    def spread_start(ph, z, src, dst):
+        row_send(ph, z, lambda peer: src.at[z, peer], lambda j: dst.at[z, r])
+        dst[z, r] = src[z, r]
+
+    def spread_finish(ph, z, dst):
+        finish(ph, z, dst.at[z, pl.ds(0, R - 1)])
+
+    def gather_start(ph, z, buf):
         for j in range(1, C):
-            yield remote(ph, z, j - 1, src, dst, {'col': lax.rem(c + j, C)})
-
-    def core_copies(ph, z, src, dst):
-        yield remote(ph, z, 0, src, dst, {'row': r + 1 - 2 * core})
-
-    def start(copies):
-        for cp in copies:
-            cp.start()
-
-    def finish(copies):
-        cps = list(copies)
-        for cp in cps:
-            cp.wait_recv()
-        for cp in cps:
-            cp.wait_send()
-
-    def spread(ph, z, src, dst):
-        return row_copies(ph, z, lambda peer: src.at[z, peer], lambda j: dst.at[z, r])
-
-    def spread_start(ph, z, src, dst):
-        start(spread(ph, z, src, dst))
-        dst[z, r] = src[z, r]
-
-    def gather(ph, z, buf):
-        return col_copies(ph, z, buf.at[z, mine], buf.at[z, mine])
-
-    def core_sum(ph, z, sb, pr):
-        return core_copies(ph, z, sb.at[z, 1 - core], pr.at[z])
-
-    def chip_sum(ph, z, sb, rb):
-        return chip_copies(ph, z, lambda peer: sb.at[z, core, peer], lambda j: rb.at[z, j - 1])
-
-    def row_sum(ph, z, sb, rb):
-        return row_copies(ph, z, lambda peer: sb.at[z, lax.rem(peer, CORES), lax.div(peer, CORES)], lambda j: rb.at[z, j - 1])
+            remote(ph, z, buf.at[z, mine], buf.at[z, mine], {'col': lax.rem(c + j, C)})
+
+    def gather_finish(ph, z, buf):
+        finish(ph, z, buf.at[z, pl.ds(0, (C - 1) * HALVES)])
 
     def sum_start(ph, z, sb, pr, rb):
-        start(core_sum(PRE[ph], z, sb, pr) if PRE[ph] is not None else row_sum(ph, z, sb, rb))
+        if PRE[ph] is not None:
+            remote(PRE[ph], z, sb.at[z, 1 - core], pr.at[z], {'row': r + 1 - 2 * core})
+        else:
+            row_send(ph, z, lambda peer: sb.at[z, lax.rem(peer, CORES), lax.div(peer, CORES)], lambda j: rb.at[z, j - 1])
 
     def sum_middle(ph, z, sb, pr, rb, tiles):
         if PRE[ph] is None:
             return
-        finish(core_sum(PRE[ph], z, sb, pr))
+        finish(PRE[ph], z, pr.at[z])
         width = sb.shape[-1] // tiles
 
         def add(t, carry):
@@ -134,10 +113,12 @@
             return carry
 
         lax.fori_loop(0, tiles, add, 0)
-        start(chip_sum(ph, z, sb, rb))
+        for j in range(1, XS):
+            peer = lax.rem(chip + j, XS)
+            remote(ph, z, sb.at[z, core, peer], rb.at[z, j - 1], {'row': peer * CORES + core})
 
     def sum_finish(ph, z, sb, rb):
-        finish(chip_sum(ph, z, sb, rb) if PRE[ph] is not None else row_sum(ph, z, sb, rb))
+        finish(ph, z, rb.at[z])
 
     def total(ph, z, sb, rb, sl):
         a = sb[z, core, chip, :, sl].astype(F32)
@@ -190,21 +171,18 @@
     vn_ref[...] = jnp.zeros_like(vn_ref)
     pl.semaphore_wait(barrier, R + C - 2)
 
-    def gain_copies():
-        return row_copies(GAIN, 0, lambda peer: gain_ref, lambda j: gains.at[r])
-
     for z in range(STREAMS):
         spread_start(X_INIT, z, xb, x)
         if z == 0:
-            start(gain_copies())
+            row_send(GAIN, 0, lambda peer: gain_ref, lambda j: gains.at[r])
     gains[r] = gain_ref[...]
     for layer in range(1, L):
         for i in range(len(pairs)):
             fetch(layer, i).start()
     for z in range(STREAMS):
-        finish(spread(X_INIT, z, xb, x))
+        spread_finish(X_INIT, z, x)
         if z == 0:
-            finish(gain_copies())
+            finish(GAIN, 0, gains.at[pl.ds(0, R - 1)])
         norm(z, 0, None)
         spread_start(N_ATTN, z, ns, nb)
 
@@ -221,7 +199,7 @@
 
     def layer_body(l, carry):
         def qkv(z):
-            finish(spread(N_ATTN, z, ns, nb))
+            spread_finish(N_ATTN, z, nb)
             if z == 0:
                 wwait(l, 0, 1, 2)
             n = nb[z].reshape(ALL, WB)
@@ -287,10 +265,10 @@
             for h in range(QH):
                 o = jnp.concatenate([os[:, s * 8 + h, :] for s in range(STEPS)], axis=0)
                 ago[z, own + h // per, :, (h % per) * HD:(h % per + 1) * HD] = o.astype(BF16)
-            start(gather(O_COL, z, ago))
+            gather_start(O_COL, z, ago)
 
         def o_row(z):
-            finish(gather(O_COL, z, ago))
+            gather_finish(O_COL, z, ago)
             spread_start(O_ROW, z, ago, no)
 
         def project(act, z, w, depth, ph):
@@ -301,7 +279,7 @@
             sum_start(ph, z, sbo, pro, rbo)
 
         def out(z):
-            finish(spread(O_ROW, z, ago, no))
+            spread_finish(O_ROW, z, no)
             if z == 0:
                 wwait(l, 5)
             project(no, z, wo, WB, OUT_B)
@@ -311,15 +289,15 @@
             for h in range(HALVES):
                 a = total(ph, z, sbo, rbo, slice(h * WB, (h + 1) * WB))
                 x[z, own + h] = (x[z, own + h].astype(F32) + a).astype(BF16)
-            start(gather(ph_col, z, x))
+            gather_start(ph_col, z, x)
 
         def mlp_norm(z):
-            finish(gather(X_MID, z, x))
+            gather_finish(X_MID, z, x)
             norm(z, L + l, None)
             spread_start(N_MLP, z, ns, nb)
 
         def gate_up(z):
-            finish(spread(N_MLP, z, ns, nb))
+            spread_finish(N_MLP, z, nb)
             if z == 0:
                 wwait(l, 6, 7)
 
@@ -348,20 +326,20 @@
                 return carry
 
             lax.fori_loop(0, 4, body, 0)
-            start(gather(A_COL, z, aga))
+            gather_start(A_COL, z, aga)
 
         def a_row(z):
-            finish(gather(A_COL, z, aga))
+            gather_finish(A_COL, z, aga)
             spread_start(A_ROW, z, aga, na)
 
         def down(z):
-            finish(spread(A_ROW, z, aga, na))
+            spread_finish(A_ROW, z, na)
             if z == 0:
                 wwait(l, 8)
             project(na, z, wd, half, DOWN_B)
 
         def end_norm(z):
-            finish(gather(X_END, z, x))
+            gather_finish(X_END, z, x)
             norm(z, l + 1, l == L - 1)
             spread_start(N_ATTN, z, ns, nb)
 
@@ -377,7 +355,7 @@
 
     lax.fori_loop(0, L, layer_body, 0)
     for z in range(STREAMS):
-        finish(spread(N_ATTN, z, ns, nb))
+        spread_finish(N_ATTN, z, nb)
     for b in range(R):
         v = [nb[z, b].astype(F32) for z in range(STREAMS)]
         for s, out in enumerate((out0, out1)):
@@ -478,7 +456,7 @@
             ((Z, CORES, XS, TOK, OUTW), BF16), ((Z, XS, TOK, OUTW), BF16), ((Z, slots(OUT_B), TOK, OUTW), BF16),
             ((Z, CORES, XS, TOK, N2), BF16), ((Z, XS, TOK, N2), BF16), ((Z, slots(GU_B), TOK, N2), BF16),
             ((Z, R, TOK, FF // HALVES), BF16), ((Z, R, TOK, FF // HALVES), BF16))]
-        scratch += [pltpu.SemaphoreType.DMA((PHASES, Z, R - 1))] * 2 + [pltpu.SemaphoreType.DMA((L, 9))]
+        scratch += [pltpu.SemaphoreType.DMA((PHASES, Z))] * 2 + [pltpu.SemaphoreType.DMA((L, 9))]
         dims = dict(R=R, C=C, L=L, D=WB * R, HD=HD)
         out_0, out_1, k_new, v_new = pl.pallas_call(
             functools.partial(decode_kernel, dims),

time: 182 us -> 162 us (0.89)
  Pallas kernels: 181 us -> 161 us
    pallas_call x1, Pallas kernels: 168 us -> 149 us  [device_program(): pl.pallas_call(functools.partial(decode_kernel, dims), out_shape=(jax.Sha...]
where the time goes in v4:
time: 162 us
  Pallas kernels  161 us (99%)
    pallas_call x1, Pallas kernels, device_program(): pl.pallas_call(functools.partial(decode_kernel, dims), out_shape=(jax.Sha...  149 us
    pallas_call x1, Pallas kernels, device_program(): pl.pallas_call(functools.partial(cache_kernel, KH), out_shape=(jax.ShapeD...  12.4 us

profile of v4, /device:TPU:97, one launch (start us, length us, event | category | flops | bytes accessed | tf_op | source)
XLA Modules:
  0.0 161.7 jit_solution(5441860809138716136)
XLA Ops:
  0.6 148.6 %decode.1 = (bf16[128,384]{1,0:T(8,128)(2,1)}, bf16[128,384]{1,0:T(8,128)(2,1)}, f32[2,16,8,128]{3,2,1,0:T(8,128)}, f32[2,16,8,128]{3,2,1,0:T(8,128)}) custom-call(bf16[128,384]{1,0:T(8,128)(2,1)} %h0.1, bf16[128,384]{1,0:T(8,128)(2,1)} %h1.1, s32[16]{0:T(128)} %pos_ref.1, s32[16]{0:T(128)} %len_ref.3, bf16[2,384]{1,0:T(2,128)(2,1)} %ga_ref.1, ...), custom_call_target="tpu_custom_call" | custom-call | tf_op jit(solution)/shard_map/decode/pallas_call | solution.py:461
  149.3 12.4 %cache_update.1 = (bf16[2,16,1024,128]{3,2,1,0:T(8,128)(2,1)}, bf16[2,16,1024,128]{3,2,1,0:T(8,128)(2,1)}, bf16[128,384]{1,0:T(8,128)(2,1)}, bf16[128,384]{1,0:T(8,128)(2,1)}) custom-call(s32[16]{0:T(128)} %len_ref.3, f32[2,16,8,128]{3,2,1,0:T(8,128)} %get-tuple-element.12.kn_h, f32[2,16,8,128]{3,2,1,0:T(8,128)} %get-tuple-element.13.vn_h, ...), custom_call_target="tpu_custom_call" | custom-call | tf_op jit(solution)/shard_map/cache_update/pallas_call | solution.py:476

commit v5 on v4

--- a/solution.py
+++ b/solution.py
@@ -20,15 +20,15 @@
 COPY_GROUPS = 4
 STREAMS = 4
 
-(X_INIT, GAIN, N_ATTN, QKV_A, QKV_B, O_COL, O_ROW, OUT_A, OUT_B, X_MID, N_MLP, GU_A, GU_B, A_COL, A_ROW, DOWN_A, DOWN_B,
- X_END, PHASES) = range(19)
+(X_INIT, SQUARES, GAIN, N_ATTN, QKV_A, QKV_B, O_COL, O_ROW, OUT_A, OUT_B, X_MID, N_MLP, GU_A, GU_B, A_COL, A_ROW, DOWN_A, DOWN_B,
+ X_END, PHASES) = range(20)
 PRE = {QKV_B: None, GU_B: GU_A, OUT_B: None, DOWN_B: None}
 
 
 def decode_kernel(dims, h0, h1, pos_ref, len_ref, ga_ref, gm_ref, wq_h, wk_h, wv_h, wo_h, wg_h, wu_h, wd_h, ck_h, cv_h,
-                  out0, out1, kn_ref, vn_ref,
-                  wq, wk, wv, wo, wg, wu, wd, ck, cv,
-                  cos_ref, sin_ref, gain_ref, xb, x, gains, ns, nb, sbq, prq, rbq, qs, sn, pn, os, ago, no, sbo, pro, rbo, sbg, prg, rbg, aga, na,
+                  out0, out1, kn_ref, vn_ref, ck, cv,
+                  wq, wk, wv, wo, wg, wu, wd,
+                  cos_ref, sin_ref, gain_ref, sq, sqs, xb, x, gains, ns, nb, sbq, prq, rbq, qs, sn, pn, os, ago, no, sbo, pro, rbo, sbg, prg, rbg, aga, na,
                   ssem, rsem, wsem):
     R, C, L, D = dims['R'], dims['C'], dims['L'], dims['D']
     HD = dims['HD']
@@ -139,9 +139,7 @@
         scale = lax.rsqrt(ss / D + EPS)
         for k in range(R):
             xk = x[z, k].astype(F32)
-            n = xk * scale * gains[k, pl.ds(gi, 1), :]
-            if last is not None:
-                n = jnp.where(last, xk, n)
+            n = xk if last else xk * scale * gains[k, gi:gi + 1, :]
             ns[z, k] = n.astype(BF16)
 
     gain_ref[...] = jnp.zeros_like(gain_ref)
@@ -171,20 +169,34 @@
     vn_ref[...] = jnp.zeros_like(vn_ref)
     pl.semaphore_wait(barrier, R + C - 2)
 
+    group = 128 // ALL
+    tok = lax.broadcasted_iota(jnp.int32, (ALL, 128), 0)
+    spot = lax.broadcasted_iota(jnp.int32, (ALL, 128), 1)
+    line = lax.broadcasted_iota(jnp.int32, (8, 128), 0)
+    packed = jnp.zeros((8, 128), F32)
+    for z in range(STREAMS):
+        xz = xb[z].astype(F32).reshape(ALL, WB)
+        ss = jnp.sum(xz * xz, axis=-1, keepdims=True)
+        lanes = jnp.sum(jnp.where(spot == tok + (z % group) * ALL, ss, 0.0), axis=0, keepdims=True)
+        packed = packed + jnp.where(line == z // group, lanes, 0.0)
+    sq[...] = packed
+    row_send(SQUARES, 0, lambda peer: sq, lambda j: sqs.at[r])
+    sqs[r] = sq[...]
+    row_send(GAIN, 0, lambda peer: gain_ref, lambda j: gains.at[r])
+    gains[r] = gain_ref[...]
     for z in range(STREAMS):
         spread_start(X_INIT, z, xb, x)
-        if z == 0:
-            row_send(GAIN, 0, lambda peer: gain_ref, lambda j: gains.at[r])
-    gains[r] = gain_ref[...]
     for layer in range(1, L):
         for i in range(len(pairs)):
             fetch(layer, i).start()
+    finish(SQUARES, 0, sqs.at[pl.ds(0, R - 1)])
+    squares = jnp.sum(sqs[...], axis=0)
     for z in range(STREAMS):
-        spread_finish(X_INIT, z, x)
-        if z == 0:
-            finish(GAIN, 0, gains.at[pl.ds(0, R - 1)])
-        norm(z, 0, None)
-        spread_start(N_ATTN, z, ns, nb)
+        row = squares[z // group:z // group + 1, :]
+        ss = jnp.sum(jnp.where(spot == tok + (z % group) * ALL, row, 0.0), axis=-1, keepdims=True)
+        scale = lax.rsqrt(ss / D + EPS)
+        n = xb[z].astype(F32).reshape(ALL, WB) * scale * gain_ref[0:1, :]
+        nb[z] = n.reshape(R, TOK, WB).astype(BF16)
 
     rows = SZ * 16
     sc = HD ** -0.5
@@ -197,9 +209,10 @@
     tile = FF // 4
     half = FF // HALVES
 
-    def layer_body(l, carry):
+    for l in range(L):
         def qkv(z):
-            spread_finish(N_ATTN, z, nb)
+            if l > 0:
+                spread_finish(N_ATTN, z, nb)
             if z == 0:
                 wwait(l, 0, 1, 2)
             n = nb[z].reshape(ALL, WB)
@@ -209,11 +222,12 @@
                 col += width
             sum_start(QKV_B, z, sbq, prq, rbq)
 
-        def qkv_middle(z):
-            sum_middle(QKV_B, z, sbq, prq, rbq, 2)
-
         def attention(z):
             sum_finish(QKV_B, z, sbq, rbq)
+            if l == 0:
+                spread_finish(X_INIT, z, x)
+                if z == 0:
+                    finish(GAIN, 0, gains.at[pl.ds(0, R - 1)])
             cos = cos_ref[z]
             sin = sin_ref[z]
 
@@ -293,7 +307,7 @@
 
         def mlp_norm(z):
             gather_finish(X_MID, z, x)
-            norm(z, L + l, None)
+            norm(z, L + l, False)
             spread_start(N_MLP, z, ns, nb)
 
         def gate_up(z):
@@ -343,7 +357,7 @@
             norm(z, l + 1, l == L - 1)
             spread_start(N_ATTN, z, ns, nb)
 
-        stages = [qkv, qkv_middle, attention, o_row, out]
+        stages = [qkv, attention, o_row, out]
         stages += [lambda z: sum_middle(OUT_B, z, sbo, pro, rbo, 1)] if PRE[OUT_B] is not None else []
         stages += [lambda z: residual(z, OUT_B, X_MID), mlp_norm, gate_up, gate_up_middle, act, a_row, down]
         stages += [lambda z: sum_middle(DOWN_B, z, sbo, pro, rbo, 1)] if PRE[DOWN_B] is not None else []
@@ -351,9 +365,7 @@
         for stage in stages:
             for z in range(STREAMS):
                 stage(z)
-        return carry
-
-    lax.fori_loop(0, L, layer_body, 0)
+
     for z in range(STREAMS):
         spread_finish(N_ATTN, z, nb)
     for b in range(R):
@@ -362,57 +374,56 @@
             out[b * SEQ:(b + 1) * SEQ] = jnp.concatenate([w[s * SZ:(s + 1) * SZ] for w in v], axis=0).astype(BF16)
 
 
-def cache_kernel(heads, len_ref, kn_h, vn_h, ck_ref, cv_ref, a0, a1, ok_ref, ov_ref, o0, o1,
-                 kn_ref, vn_ref, kbuf, vbuf, b0, b1, rsem, wsem, nsem):
+def cache_kernel(heads, len_ref, kn_ref, vn_ref, a0, a1, ck_ref, cv_ref, ok_ref, ov_ref, o0, o1,
+                 kwin, vwin, bsem, wsem, nsem):
     layers, seqs, rows, width = ck_ref.shape
+    sides = ((ck_ref, kwin, kn_ref, ok_ref), (cv_ref, vwin, vn_ref, ov_ref))
+    pass_on = [pltpu.make_async_copy(a, b, nsem.at[i]) for i, (a, b) in enumerate(((a0, o0), (a1, o1)))]
     group = seqs // COPY_GROUPS
-    sides = ((ck_ref, kbuf, kn_ref, ok_ref), (cv_ref, vbuf, vn_ref, ov_ref))
-    small = [pltpu.make_async_copy(a, b, nsem.at[i]) for i, (a, b) in enumerate(((kn_h, kn_ref), (vn_h, vn_ref), (a0, b0), (a1, b1)))]
-    pass_on = [pltpu.make_async_copy(a, b, nsem.at[4 + i]) for i, (a, b) in enumerate(((b0, o0), (b1, o1)))]
-
-    def load(k, i):
+
+    def bulk(k, i):
         at = (i // COPY_GROUPS, pl.ds((i % COPY_GROUPS) * group, group))
-        return pltpu.make_async_copy(sides[k][0].at[at], sides[k][1].at[i], rsem.at[k, i])
-
-    def save(k, i):
-        at = (i // COPY_GROUPS, pl.ds((i % COPY_GROUPS) * group, group))
-        return pltpu.make_async_copy(sides[k][1].at[i], sides[k][3].at[at], wsem.at[k, i])
+        return pltpu.make_async_copy(sides[k][0].at[at], sides[k][3].at[at], bsem.at[k, i])
+
+    def place(b):
+        at = len_ref[b] * heads
+        return at, pl.multiple_of(jnp.minimum((at // 16) * 16, rows - 32), 16)
+
+    def window(k, layer, b):
+        return pltpu.make_async_copy(sides[k][1].at[layer, b], sides[k][3].at[layer, b, pl.ds(place(b)[1], 32)], wsem.at[k, layer, b])
 
     count = layers * COPY_GROUPS
-    for cp in small:
-        cp.start()
     for i in range(count):
         for k in range(2):
-            load(k, i).start()
-    for cp in small:
-        cp.wait()
+            bulk(k, i).start()
     for cp in pass_on:
         cp.start()
-    for i in range(count):
-        layer, first = i // COPY_GROUPS, (i % COPY_GROUPS) * group
-        for k in range(2):
-            load(k, i).wait()
-
-            def patch(g, carry):
-                buf, fresh = sides[k][1], sides[k][2]
-                at = len_ref[first + g] * heads
-                base = pl.multiple_of(jnp.minimum((at // 16) * 16, rows - 32), 16)
-                win = pl.ds(base, 32)
-                idx = lax.broadcasted_iota(jnp.int32, (32, width), 0) + base - at
-                val = buf[i, g, win, :].astype(F32)
-                new = fresh[layer, first + g]
+
+    def patch(b, carry):
+        at, base = place(b)
+        idx = lax.broadcasted_iota(jnp.int32, (32, width), 0) + base - at
+        for layer in range(layers):
+            for src, win, fresh, _ in sides:
+                val = src[layer, b, pl.ds(base, 32), :].astype(F32)
+                new = fresh[layer, b]
                 for n in range(STEPS * heads):
                     val = jnp.where(idx == n, new[n:n + 1, :], val)
-                buf[i, g, win, :] = val.astype(BF16)
-                return carry
-
-            lax.fori_loop(0, group, patch, 0, unroll=True)
-            save(k, i).start()
+                win[layer, b] = val.astype(BF16)
+        return carry
+
+    lax.fori_loop(0, seqs, patch, 0, unroll=2)
+    for i in range(count):
+        for k in range(2):
+            bulk(k, i).wait()
+        for g in range(group):
+            for k in range(2):
+                window(k, i // COPY_GROUPS, (i % COPY_GROUPS) * group + g).start()
     for cp in pass_on:
         cp.wait()
-    for i in range(count):
-        for k in range(2):
-            save(k, i).wait()
+    for layer in range(layers):
+        for b in range(seqs):
+            for k in range(2):
+                window(k, layer, b).wait()
 
 
 def solution(mesh):
@@ -437,9 +448,9 @@
         cv = cache_v.reshape(L, SEQ, SLOTS, HD)
         vm = pl.BlockSpec(memory_space=pltpu.VMEM)
         smem = pl.BlockSpec(memory_space=pltpu.SMEM)
-        hbm = pl.BlockSpec(memory_space=pl.ANY)
+        hbm = pl.BlockSpec(memory_space=pltpu.HBM)
         weights = (w_query, w_key, w_value, w_out, w_gate, w_up, w_down)
-        scratch = [pltpu.VMEM(w.shape, BF16) for w in weights] + [pltpu.VMEM(ck.shape, BF16)] * 2
+        scratch = [pltpu.VMEM(w.shape, BF16) for w in weights]
         N3 = QC + 2 * KC
         N2 = 2 * FF
         OUTW = HALVES * WB
@@ -448,7 +459,7 @@
             return R - 1 if PRE[ph] is None else XS - 1
 
         scratch += [pltpu.VMEM(s, d) for s, d in (
-            ((Z, TOK, HD), F32), ((Z, TOK, HD), F32), ((8, WB), F32),
+            ((Z, TOK, HD), F32), ((Z, TOK, HD), F32), ((8, WB), F32), ((8, 128), F32), ((R, 8, 128), F32),
             ((Z, R, TOK, WB), BF16), ((Z, R, TOK, WB), BF16), ((R, 8, WB), F32), ((Z, R, TOK, WB), BF16), ((Z, R, TOK, WB), BF16),
             ((Z, CORES, XS, TOK, N3), BF16), ((Z, XS, TOK, N3), BF16), ((Z, slots(QKV_B), TOK, N3), BF16),
             ((SZ, 16, HD), F32), ((SZ, 16, SZ * 8), F32), ((SZ, 16, SZ * 8), BF16), ((SZ, 16, HD), F32),
@@ -458,31 +469,30 @@
             ((Z, R, TOK, FF // HALVES), BF16), ((Z, R, TOK, FF // HALVES), BF16))]
         scratch += [pltpu.SemaphoreType.DMA((PHASES, Z))] * 2 + [pltpu.SemaphoreType.DMA((L, 9))]
         dims = dict(R=R, C=C, L=L, D=WB * R, HD=HD)
-        out_0, out_1, k_new, v_new = pl.pallas_call(
+        out_0, out_1, k_new, v_new, kept_k, kept_v = pl.pallas_call(
             functools.partial(decode_kernel, dims),
-            out_shape=(jax.ShapeDtypeStruct(hidden_0.shape, BF16), jax.ShapeDtypeStruct(hidden_1.shape, BF16),
-                       jax.ShapeDtypeStruct((L, SEQ, 8, HD), F32), jax.ShapeDtypeStruct((L, SEQ, 8, HD), F32)),
+            out_shape=(pltpu.VMEM(hidden_0.shape, BF16), pltpu.VMEM(hidden_1.shape, BF16),
+                       pltpu.VMEM((L, SEQ, 8, HD), F32), pltpu.VMEM((L, SEQ, 8, HD), F32),
+                       pltpu.VMEM(ck.shape, BF16), pltpu.VMEM(ck.shape, BF16)),
             in_specs=[vm, vm, smem, smem, vm, vm] + [hbm] * 9,
-            out_specs=(vm, vm, vm, vm),
+            out_specs=(vm,) * 6,
             scratch_shapes=scratch,
-            compiler_params=pltpu.CompilerParams(collective_id=0, has_side_effects=True, vmem_limit_bytes=62 * 1024 * 1024),
+            compiler_params=pltpu.CompilerParams(collective_id=0, has_side_effects=True, vmem_limit_bytes=47 * 1024 * 1024),
             name='decode',
         )(hidden_0, hidden_1, positions, lengths, norm_attn, norm_mlp, *weights, ck, cv)
 
         count = L * COPY_GROUPS
-        buf = pltpu.VMEM((count, SEQ // COPY_GROUPS, SLOTS, HD), BF16)
-        fresh = pltpu.VMEM(k_new.shape, F32)
-        hidden = pltpu.VMEM(hidden_0.shape, BF16)
+        win = pltpu.VMEM((L, SEQ, 32, HD), BF16)
         ok, ov, out_0, out_1 = pl.pallas_call(
             functools.partial(cache_kernel, KH),
             out_shape=(jax.ShapeDtypeStruct(ck.shape, BF16),) * 2 + (jax.ShapeDtypeStruct(hidden_0.shape, BF16),) * 2,
-            in_specs=[smem] + [hbm] * 6,
+            in_specs=[smem] + [vm] * 6,
             out_specs=(hbm,) * 4,
-            scratch_shapes=[fresh, fresh, buf, buf, hidden, hidden, pltpu.SemaphoreType.DMA((2, count)),
-                            pltpu.SemaphoreType.DMA((2, count)), pltpu.SemaphoreType.DMA((6,))],
-            compiler_params=pltpu.CompilerParams(vmem_limit_bytes=62 * 1024 * 1024),
+            scratch_shapes=[win, win, pltpu.SemaphoreType.DMA((2, count)),
+                            pltpu.SemaphoreType.DMA((2, L, SEQ)), pltpu.SemaphoreType.DMA((2,))],
+            compiler_params=pltpu.CompilerParams(vmem_limit_bytes=8 * 1024 * 1024),
             name='cache_update',
-        )(lengths, k_new, v_new, ck, cv, out_0, out_1)
+        )(lengths, k_new, v_new, out_0, out_1, kept_k, kept_v)
         ok, ov = ok.reshape(cache_k.shape), ov.reshape(cache_v.shape)
         return out_0, out_1, ok, ov
 

time: 162 us -> 152 us (0.938)
  Pallas kernels: 161 us -> 151 us
    pallas_call x1, Pallas kernels: 149 us -> 143 us  [device_program(): pl.pallas_call(functools.partial(decode_kernel, dims), out_shape=(pltpu.V...]
    pallas_call x1, Pallas kernels: 12.4 us -> 7.74 us  [device_program(): pl.pallas_call(functools.partial(cache_kernel, KH), out_shape=(jax.ShapeD...]
where the time goes in v5:
time: 152 us
  Pallas kernels  151 us (99%)
    pallas_call x1, Pallas kernels, device_program(): pl.pallas_call(functools.partial(decode_kernel, dims), out_shape=(pltpu.V...  143 us
    pallas_call x1, Pallas kernels, device_program(): pl.pallas_call(functools.partial(cache_kernel, KH), out_shape=(jax.ShapeD...  7.74 us

profile of v5, /device:TPU:97, one launch (start us, length us, event | category | flops | bytes accessed | tf_op | source)
XLA Modules:
  0.0 152.0 jit_solution(397036737725086044)
XLA Ops:
  0.6 0.0 copy-start
  0.6 143.5 %decode.1 = (bf16[128,384]{1,0:T(8,128)(2,1)S(1)}, bf16[128,384]{1,0:T(8,128)(2,1)S(1)}, f32[2,16,8,128]{3,2,1,0:T(8,128)S(1)}, f32[2,16,8,128]{3,2,1,0:T(8,128)...) custom-call(bf16[128,384]{1,0:T(8,128)(2,1)} %h0.1, bf16[128,384]{1,0:T(8,128)(2,1)} %h1.1, ...), custom_call_target="tpu_custom_call" | custom-call | tf_op jit(solution)/shard_map/decode/pallas_call | solution.py:472
  144.1 0.0 copy-done
  144.1 7.7 %cache_update.1 = (bf16[2,16,1024,128]{3,2,1,0:T(8,128)(2,1)}, bf16[2,16,1024,128]{3,2,1,0:T(8,128)(2,1)}, bf16[128,384]{1,0:T(8,128)(2,1)}, bf16[128,384]{1,0:T(8,128)(2,1)}) custom-call(s32[16]{0:T(128)S(1)} %copy-done, f32[2,16,8,128]{3,2,1,0:T(8,128)S(1)} %get-tuple-element.14.kn_ref, f32[2,16,8,128]{3,2,1,0:T(8,128)S(1)} %get-tuple-element.15.vn_ref, ...), custom_call_target="tpu_custom_call" | custom-call | tf_op jit(solution)/shard_map/cache_update/pallas_call | solution.py:486
Async XLA Ops:
  0.6 143.5 %copy-start = (s32[16]{0:T(128)S(1)}, s32[16]{0:T(128)}, u32[]{:S(2)}) copy-start(s32[16]{0:T(128)} %len_ref.3) | copy-start | bytes 196

commit v6 on v5

--- a/solution.py
+++ b/solution.py
@@ -18,11 +18,31 @@
 
 CORES = 2
 COPY_GROUPS = 4
+PICK = 0
 STREAMS = 4
 
 (X_INIT, SQUARES, GAIN, N_ATTN, QKV_A, QKV_B, O_COL, O_ROW, OUT_A, OUT_B, X_MID, N_MLP, GU_A, GU_B, A_COL, A_ROW, DOWN_A, DOWN_B,
  X_END, PHASES) = range(20)
 PRE = {QKV_B: None, GU_B: GU_A, OUT_B: None, DOWN_B: None}
+
+
+COSTS = [(0.4, 0, 1.75, 2.8), (1.9, 1, 0.55, 2.8), (0.2, 0, 0.55, 2.8), (0.4, 0, 1.05, 2.8), (0.3, 1, 0.55, 2.8), (0.4, 0, 0.55, 2.8),
+         (1.1, 2, 0.4, 1.1), (0.2, 0, 2.8, 2.8), (0.3, 1, 1.4, 2.8), (0.2, 0, 1.4, 2.8), (0.5, 0, 1.05, 2.8), (0.3, 1, 0.55, 2.8),
+         (0.4, 0, 0.55, 2.8)]
+
+
+def stage_order(layers):
+    costs = COSTS * layers
+    ready, done, links, now, order = [0.0] * STREAMS, [0] * STREAMS, [0.0] * 3, 0.0, []
+    while min(done) < len(costs):
+        z = min((k for k in range(STREAMS) if done[k] < len(costs)), key=lambda k: (max(ready[k], now), PICK * done[k], k))
+        core, link, wire, latency = costs[done[z]]
+        now = max(now, ready[z]) + core
+        links[link] = max(links[link], now) + wire
+        ready[z] = links[link] + latency
+        order.append((done[z], z))
+        done[z] += 1
+    return order
 
 
 def decode_kernel(dims, h0, h1, pos_ref, len_ref, ga_ref, gm_ref, wq_h, wk_h, wv_h, wo_h, wg_h, wu_h, wd_h, ck_h, cv_h,
@@ -55,9 +75,13 @@
     def fetch(layer, i):
         return pltpu.make_async_copy(pairs[i][0].at[layer], pairs[i][1].at[layer], wsem.at[layer, i])
 
+    waited = set()
+
     def wwait(layer, *which):
         for i in which:
-            fetch(layer, i).wait()
+            if (layer, i) not in waited:
+                waited.add((layer, i))
+                fetch(layer, i).wait()
 
     for i in range(len(pairs)):
         fetch(0, i).start()
@@ -209,12 +233,11 @@
     tile = FF // 4
     half = FF // HALVES
 
-    for l in range(L):
+    def layer_stages(l):
         def qkv(z):
             if l > 0:
                 spread_finish(N_ATTN, z, nb)
-            if z == 0:
-                wwait(l, 0, 1, 2)
+            wwait(l, 0, 1, 2)
             n = nb[z].reshape(ALL, WB)
             col = 0
             for w, width in ((wq, QC), (wk, KC), (wv, KC)):
@@ -226,7 +249,8 @@
             sum_finish(QKV_B, z, sbq, rbq)
             if l == 0:
                 spread_finish(X_INIT, z, x)
-                if z == 0:
+                if not waited & {GAIN}:
+                    waited.add(GAIN)
                     finish(GAIN, 0, gains.at[pl.ds(0, R - 1)])
             cos = cos_ref[z]
             sin = sin_ref[z]
@@ -254,8 +278,7 @@
             vnew = vn_ref[l, seqs].reshape(SZ * 8, HD).astype(BF16)
             s_new = lax.dot_general(qall, knew, NT, preferred_element_type=F32) * sc
             sn[...] = jnp.where(new_ok, s_new, -jnp.inf).reshape(SZ, 16, SZ * 8)
-            if z == 0:
-                wwait(l, 3, 4)
+            wwait(l, 3, 4)
             kvrow = jnp.where(lax.broadcasted_iota(jnp.int32, (16, SLOTS), 0) % 8 >= G, 1, 0)
             kcol = lax.broadcasted_iota(jnp.int32, (16, SLOTS), 1)
             parity = (kcol % KH) == kvrow
@@ -294,8 +317,7 @@
 
         def out(z):
             spread_finish(O_ROW, z, no)
-            if z == 0:
-                wwait(l, 5)
+            wwait(l, 5)
             project(no, z, wo, WB, OUT_B)
 
         def residual(z, ph, ph_col):
@@ -312,8 +334,7 @@
 
         def gate_up(z):
             spread_finish(N_MLP, z, nb)
-            if z == 0:
-                wwait(l, 6, 7)
+            wwait(l, 6, 7)
 
             def body(t, carry):
                 off = pl.multiple_of(t * tile, tile)
@@ -348,8 +369,7 @@
 
         def down(z):
             spread_finish(A_ROW, z, na)
-            if z == 0:
-                wwait(l, 8)
+            wwait(l, 8)
             project(na, z, wd, half, DOWN_B)
 
         def end_norm(z):
@@ -362,10 +382,11 @@
         stages += [lambda z: residual(z, OUT_B, X_MID), mlp_norm, gate_up, gate_up_middle, act, a_row, down]
         stages += [lambda z: sum_middle(DOWN_B, z, sbo, pro, rbo, 1)] if PRE[DOWN_B] is not None else []
         stages += [lambda z: residual(z, DOWN_B, X_END), end_norm]
-        for stage in stages:
-            for z in range(STREAMS):
-                stage(z)
-
+        return stages
+
+    stages = [stage for l in range(L) for stage in layer_stages(l)]
+    for i, z in stage_order(L):
+        stages[i](z)
     for z in range(STREAMS):
         spread_finish(N_ATTN, z, nb)
     for b in range(R):

time: 152 us -> 145 us (0.954)
  Pallas kernels: 151 us -> 144 us
    pallas_call x1, Pallas kernels: 143 us -> 136 us  [device_program(): pl.pallas_call(functools.partial(decode_kernel, dims), out_shape=(pltpu.V...]
where the time goes in v6:
time: 145 us
  Pallas kernels  144 us (99%)
    pallas_call x1, Pallas kernels, device_program(): pl.pallas_call(functools.partial(decode_kernel, dims), out_shape=(pltpu.V...  136 us
    pallas_call x1, Pallas kernels, device_program(): pl.pallas_call(functools.partial(cache_kernel, KH), out_shape=(jax.ShapeD...  7.74 us

profile of v6, /device:TPU:97, one launch (start us, length us, event | category | flops | bytes accessed | tf_op | source)
XLA Modules:
  0.0 144.7 jit_solution(1185814784425416420)
XLA Ops:
  0.6 0.0 copy-start
  0.6 136.1 %decode.1 = (bf16[128,384]{1,0:T(8,128)(2,1)S(1)}, bf16[128,384]{1,0:T(8,128)(2,1)S(1)}, f32[2,16,8,128]{3,2,1,0:T(8,128)S(1)}, f32[2,16,8,128]{3,2,1,0:T(8,128)...) custom-call(bf16[128,384]{1,0:T(8,128)(2,1)} %h0.1, bf16[128,384]{1,0:T(8,128)(2,1)} %h1.1, ...), custom_call_target="tpu_custom_call" | custom-call | tf_op jit(solution)/shard_map/decode/pallas_call | solution.py:493
  136.8 0.0 copy-done
  136.8 7.7 %cache_update.1 = (bf16[2,16,1024,128]{3,2,1,0:T(8,128)(2,1)}, bf16[2,16,1024,128]{3,2,1,0:T(8,128)(2,1)}, bf16[128,384]{1,0:T(8,128)(2,1)}, bf16[128,384]{1,0:T(8,128)(2,1)}) custom-call(s32[16]{0:T(128)S(1)} %copy-done, f32[2,16,8,128]{3,2,1,0:T(8,128)S(1)} %get-tuple-element.14.kn_ref, f32[2,16,8,128]{3,2,1,0:T(8,128)S(1)} %get-tuple-element.15.vn_ref, ...), custom_call_target="tpu_custom_call" | custom-call | tf_op jit(solution)/shard_map/cache_update/pallas_call | solution.py:507
Async XLA Ops:
  0.6 136.2 %copy-start = (s32[16]{0:T(128)S(1)}, s32[16]{0:T(128)}, u32[]{:S(2)}) copy-start(s32[16]{0:T(128)} %len_ref.3) | copy-start | bytes 196

commit v7 on v6

--- a/solution.py
+++ b/solution.py
@@ -29,6 +29,10 @@
 COSTS = [(0.4, 0, 1.75, 2.8), (1.9, 1, 0.55, 2.8), (0.2, 0, 0.55, 2.8), (0.4, 0, 1.05, 2.8), (0.3, 1, 0.55, 2.8), (0.4, 0, 0.55, 2.8),
          (1.1, 2, 0.4, 1.1), (0.2, 0, 2.8, 2.8), (0.3, 1, 1.4, 2.8), (0.2, 0, 1.4, 2.8), (0.5, 0, 1.05, 2.8), (0.3, 1, 0.55, 2.8),
          (0.4, 0, 0.55, 2.8)]
+
+
+def far_first(n):
+    return sorted(range(1, n), key=lambda j: -min(j, n - j))
 
 
 def stage_order(layers):
@@ -101,7 +105,7 @@
         pltpu.make_async_copy(received, received, ssem.at[ph, z]).wait()
 
     def row_send(ph, z, src, dst):
-        for j in range(1, R):
+        for j in far_first(R):
             peer = lax.rem(r + j, R)
             remote(ph, z, src(peer), dst(j), {'row': peer})
 
@@ -113,7 +117,7 @@
         finish(ph, z, dst.at[z, pl.ds(0, R - 1)])
 
     def gather_start(ph, z, buf):
-        for j in range(1, C):
+        for j in far_first(C):
             remote(ph, z, buf.at[z, mine], buf.at[z, mine], {'col': lax.rem(c + j, C)})
 
     def gather_finish(ph, z, buf):
@@ -137,7 +141,7 @@
             return carry
 
         lax.fori_loop(0, tiles, add, 0)
-        for j in range(1, XS):
+        for j in far_first(XS):
             peer = lax.rem(chip + j, XS)
             remote(ph, z, sb.at[z, core, peer], rb.at[z, j - 1], {'row': peer * CORES + core})
 
@@ -230,7 +234,7 @@
     kvh = jnp.where(ri % 8 >= G, 1, 0)
     new_ok = (ri // 16 == ci // 8) & (slot < STEPS * KH) & (slot % KH == kvh) & (slot // KH <= (ri % 16) // 8)
     per = QH // HALVES
-    tile = FF // 4
+    tile = FF // 2
     half = FF // HALVES
 
     def layer_stages(l):
@@ -343,7 +347,7 @@
                     put(sbg, z, pl.ds(off + k * FF, tile), jnp.dot(n, w[l, :, pl.ds(off, tile)], preferred_element_type=F32))
                 return carry
 
-            lax.fori_loop(0, 4, body, 0)
+            lax.fori_loop(0, FF // tile, body, 0)
             sum_start(GU_B, z, sbg, prg, rbg)
 
         def gate_up_middle(z):
@@ -360,7 +364,7 @@
                 aga[z, own + t // per_half, :, pl.ds(pl.multiple_of((t % per_half) * tile, tile), tile)] = (jax.nn.silu(g) * u).astype(BF16)
                 return carry
 
-            lax.fori_loop(0, 4, body, 0)
+            lax.fori_loop(0, FF // tile, body, 0)
             gather_start(A_COL, z, aga)
 
         def a_row(z):

time: 145 us -> 142 us (0.979)
  Pallas kernels: 144 us -> 141 us
    pallas_call x1, Pallas kernels: 136 us -> 134 us  [device_program(): pl.pallas_call(functools.partial(decode_kernel, dims), out_shape=(pltpu.V...]
where the time goes in v7:
time: 142 us
  Pallas kernels  141 us (99%)
    pallas_call x1, Pallas kernels, device_program(): pl.pallas_call(functools.partial(decode_kernel, dims), out_shape=(pltpu.V...  134 us
    pallas_call x1, Pallas kernels, device_program(): pl.pallas_call(functools.partial(cache_kernel, KH), out_shape=(jax.ShapeD...  7.74 us

profile of v7, /device:TPU:97, one launch (start us, length us, event | category | flops | bytes accessed | tf_op | source)
XLA Modules:
  0.0 142.2 jit_solution(11984385666333330188)
XLA Ops:
  0.6 0.0 copy-start
  0.6 133.6 %decode.1 = (bf16[128,384]{1,0:T(8,128)(2,1)S(1)}, bf16[128,384]{1,0:T(8,128)(2,1)S(1)}, f32[2,16,8,128]{3,2,1,0:T(8,128)S(1)}, f32[2,16,8,128]{3,2,1,0:T(8,128)...) custom-call(bf16[128,384]{1,0:T(8,128)(2,1)} %h0.1, bf16[128,384]{1,0:T(8,128)(2,1)} %h1.1, ...), custom_call_target="tpu_custom_call" | custom-call | tf_op jit(solution)/shard_map/decode/pallas_call | solution.py:497
  134.3 0.0 copy-done
  134.3 7.7 %cache_update.1 = (bf16[2,16,1024,128]{3,2,1,0:T(8,128)(2,1)}, bf16[2,16,1024,128]{3,2,1,0:T(8,128)(2,1)}, bf16[128,384]{1,0:T(8,128)(2,1)}, bf16[128,384]{1,0:T(8,128)(2,1)}) custom-call(s32[16]{0:T(128)S(1)} %copy-done, f32[2,16,8,128]{3,2,1,0:T(8,128)S(1)} %get-tuple-element.14.kn_ref, f32[2,16,8,128]{3,2,1,0:T(8,128)S(1)} %get-tuple-element.15.vn_ref, ...), custom_call_target="tpu_custom_call" | custom-call | tf_op jit(solution)/shard_map/cache_update/pallas_call | solution.py:511
Async XLA Ops:
  0.6 133.6 %copy-start = (s32[16]{0:T(128)S(1)}, s32[16]{0:T(128)}, u32[]{:S(2)}) copy-start(s32[16]{0:T(128)} %len_ref.3) | copy-start | bytes 196
